TPU v7x, 32 devices: a whole 2x2x4 slice. The times are simulated.
32 devices in a mesh: section: 2 (over y), dp: 4 (over x, core), mp: 4 (over z).
Axes of the slice: x: 2, y: 2, z: 4, core: 2. Of those that a mesh axis runs over, the one named last changes fastest.
Arguments:
- patches: bfloat16 [4096, 1280], P(('section', 'dp')), may hold values from -6 to 6
- patch_counts: int32 [16], P(('section', 'dp')), may hold values from 64 to 256, as said below
- dest_rows: int32 [1024], P(('section', 'dp')), may hold values from 0 to 4095, as said below
- qkv_weight: bfloat16 [1280, 3, 1280], P(None, None, 'mp'), may hold values from -1 to 1
- out_weight: bfloat16 [1280, 1280], P('mp'), may hold values from -0.15625 to 0.15625
- attn_gain: bfloat16 [1280], replicated, may hold values from 0.25 to 1.75
- merge_gain: bfloat16 [1280], replicated, may hold values from 0.25 to 1.75
- fc1_weight: bfloat16 [5120, 5120], P('mp', ('section', 'dp')), may hold values from -0.078125 to 0.078125
- fc1_bias: bfloat16 [5120], P(('section', 'dp')), may hold values from -3 to 3
- fc2_weight: bfloat16 [5120, 8192], P(('section', 'dp'), 'mp'), may hold values from -0.078125 to 0.078125
- fc2_bias: bfloat16 [8192], P('mp'), may hold values from -3 to 3
- text_embeds: bfloat16 [4096, 8192], P(('section', 'dp'), 'mp'), may hold values from -6 to 6
- section_hidden: bfloat16 [4096, 8192], P(('section', 'dp'), 'mp'), may hold values from -80 to 80
- llm_gain: bfloat16 [8192], P('mp'), may hold values from 0.25 to 1.75
Outputs:
- sequence_embeds: bfloat16 [4096, 8192], P(('section', 'dp'), 'mp')
- layer_inputs: bfloat16 [4096, 8192], P(('section', 'dp'), 'mp')
Inputs may be any that keep to these rules, and one draw needn't show every extreme that they name: `patch_counts`: multiples of 4; a tile's patches fill the first slots of its block. `dest_rows`: all rows differ. Each group's merged slots form runs of 16 consecutive slots (aligned); a run goes to one sequence slice (row // 512, numbered in section-major order), different runs of a group to different slices. Rows of slots that are not live are never written.
All inputs are finite; a program needn't handle non-finite values.
Results may differ from a plain program's by a relative error of at most 0.0055.
Values may be sent and summed in bfloat16 or wider, within the bound.
A program may use at most 128 MiB of HBM per device.

v0:
```python
import functools
import math

import jax
import jax.numpy as jnp
from jax import lax
from jax.experimental import pallas as pl
from jax.experimental.pallas import tpu as pltpu
from jax.sharding import PartitionSpec as P

HEAD_DIM = 80
HID = 8192


vit_eps = 1e-06
llm_eps = 1e-06


def from_behind(value, axis, steps):
    count = lax.axis_size(axis)
    first, last = (max(0, -steps), min(count, count - steps))
    return lax.ppermute(value, axis, [(source, source + steps) for source in range(first, last)])


def layer_norm(values, gain):
    centred = values.astype(jnp.float32)
    centred = centred - jnp.mean(centred, axis=-1, keepdims=True)
    variance = jnp.mean(centred * centred, axis=-1, keepdims=True)
    return centred * lax.rsqrt(variance + vit_eps) * gain.astype(jnp.float32)


VMEM_LIMIT = 60 * 1024 * 1024
KERNEL_BYTES = 8 * 1024 * 1024


def vmem_call(kernel, out, scratch, sent_bytes, ident, *operands):
    return pl.pallas_call(
        kernel,
        out_shape=out,
        in_specs=[pl.BlockSpec(memory_space=pltpu.VMEM)] * len(operands),
        out_specs=pl.BlockSpec(memory_space=pltpu.VMEM),
        scratch_shapes=scratch,
        cost_estimate=pl.CostEstimate(
            flops=sent_bytes * 20000, bytes_accessed=sent_bytes * 2, transcendentals=0
        ),
        compiler_params=pltpu.CompilerParams(
            collective_id=ident, has_side_effects=True, vmem_limit_bytes=VMEM_LIMIT
        ),
    )(*operands)


def exchange_kernel(count, spread, x_ref, o_ref, send_sem, recv_sem, own_sem):
    me = lax.axis_index("mp")
    barrier = pltpu.get_barrier_semaphore()
    for step in range(1, count):
        peer = lax.rem(me + step, count)
        pl.semaphore_signal(
            barrier, inc=1, device_id={"mp": peer}, device_id_type=pl.DeviceIdType.MESH
        )
    pl.semaphore_wait(barrier, count - 1)
    copies = []
    for step in sorted(range(1, count), key=lambda s: -min(s, count - s)):
        peer = lax.rem(me + step, count)
        copy = pltpu.make_async_remote_copy(
            src_ref=x_ref.at[peer] if spread else x_ref,
            dst_ref=o_ref.at[me],
            send_sem=send_sem.at[step - 1],
            recv_sem=recv_sem.at[step - 1],
            device_id={"mp": peer},
            device_id_type=pl.DeviceIdType.MESH,
        )
        copy.start()
        copies.append(copy)
    own = pltpu.make_async_copy(x_ref.at[me] if spread else x_ref, o_ref.at[me], own_sem)
    own.start()
    own.wait()
    for copy in copies:
        copy.wait()


def relay_kernel(count, x_ref, o_ref, send_sem, recv_sem, own_sem):
    me = lax.axis_index("mp")
    barrier = pltpu.get_barrier_semaphore()
    for step in range(1, count):
        peer = lax.rem(me + step, count)
        pl.semaphore_signal(
            barrier, inc=1, device_id={"mp": peer}, device_id_type=pl.DeviceIdType.MESH
        )
    pl.semaphore_wait(barrier, count - 1)
    own = pltpu.make_async_copy(x_ref, o_ref.at[me], own_sem)
    own.start()

    def hop(way, step):
        owner = lax.rem(me - way * step + count, count)
        return pltpu.make_async_remote_copy(
            src_ref=o_ref.at[owner] if step else x_ref,
            dst_ref=o_ref.at[owner],
            send_sem=send_sem.at[(way + 1) // 2, step],
            recv_sem=recv_sem.at[(way + 1) // 2, step],
            device_id={"mp": lax.rem(me + way + count, count)},
            device_id_type=pl.DeviceIdType.MESH,
        )

    def holds(way, step):
        return me >= step if way > 0 else me + step < count

    def sends(way):
        return me < count - 1 if way > 0 else me > 0

    for step in range(count):
        for way in (1, -1):
            if step:

                @pl.when(holds(way, step))
                def _():
                    owner = lax.rem(me - way * step + count, count)
                    pltpu.make_async_remote_copy(
                        src_ref=x_ref,
                        dst_ref=o_ref.at[owner],
                        send_sem=send_sem.at[(way + 1) // 2, step - 1],
                        recv_sem=recv_sem.at[(way + 1) // 2, step - 1],
                        device_id={"mp": lax.rem(me - way + count, count)},
                        device_id_type=pl.DeviceIdType.MESH,
                    ).wait_recv()

            if step < count - 1:

                @pl.when(jnp.logical_and(holds(way, step), sends(way)))
                def _():
                    hop(way, step).start()

    own.wait()
    for step in range(count - 1):
        for way in (1, -1):

            @pl.when(jnp.logical_and(holds(way, step), sends(way)))
            def _():
                hop(way, step).wait_send()


def relay_mp(value, ident):
    count = lax.axis_size("mp")
    return vmem_call(
        functools.partial(relay_kernel, count),
        jax.ShapeDtypeStruct((count,) + value.shape, value.dtype),
        [
            pltpu.SemaphoreType.DMA((2, count - 1)),
            pltpu.SemaphoreType.DMA((2, count - 1)),
            pltpu.SemaphoreType.DMA,
        ],
        count * value.size * value.dtype.itemsize,
        ident,
        value,
    )


def exchange_mp(value, spread, ident):
    count = lax.axis_size("mp")
    shape = value.shape if spread else (count,) + value.shape
    size = math.prod(shape) * value.dtype.itemsize
    return vmem_call(
        functools.partial(exchange_kernel, count, spread),
        jax.ShapeDtypeStruct(shape, value.dtype),
        [
            pltpu.SemaphoreType.DMA((count - 1,)),
            pltpu.SemaphoreType.DMA((count - 1,)),
            pltpu.SemaphoreType.DMA,
        ],
        size,
        ident,
        value,
    )


def sum_scatter_mp(blocks, ident):
    return jnp.sum(exchange_mp(blocks, True, ident).astype(jnp.float32), axis=0)


def gather_mp(value):
    got = relay_mp(value, 2)
    return got.reshape((-1,) + value.shape[1:])


def total_mp(value):
    return jnp.sum(exchange_mp(value.reshape(-1, 128), False, 3), axis=0).reshape(-1)


def flip(index, bit):
    return index + bit * (1 - 2 * (index // bit % 2))


def group_bits():
    outer = [("dp", 1 << k) for k in range(1, lax.axis_size("dp").bit_length() - 1)]
    outer += [("section", 1 << k) for k in range(lax.axis_size("section").bit_length() - 1)]
    return outer, ("dp", 1)


def meets(axis, bit):
    return {axis: flip(lax.axis_index(axis), bit)}


def group_at(mask):
    spots = {axis: lax.axis_index(axis) for axis in ("section", "dp")}
    for axis, bit in mask:
        spots[axis] = flip(spots[axis], bit)
    return spots["section"] * lax.axis_size("dp") + spots["dp"]


def greet(bits):
    barrier = pltpu.get_barrier_semaphore()
    for axis, bit in bits:
        pl.semaphore_signal(
            barrier, inc=1, device_id=meets(axis, bit), device_id_type=pl.DeviceIdType.MESH
        )
    pl.semaphore_wait(barrier, len(bits))


def gather_kernel(x_ref, o_ref, send_sem, recv_sem, own_sem):
    outer, last = group_bits()
    greet(outer + [last])
    half = x_ref.shape[1] // 2
    sent, waiting = [], []
    slots = iter(range(send_sem.shape[0]))

    def pass_on(mask, stage, part, order):
        cols = pl.ds(part * half, half)
        spot = group_at(mask)
        source = o_ref.at[spot, :, cols] if mask else x_ref.at[:, cols]
        for later in range(stage, len(order)):
            slot = next(slots)
            copy = pltpu.make_async_remote_copy(
                src_ref=source,
                dst_ref=o_ref.at[spot, :, cols],
                send_sem=send_sem.at[slot],
                recv_sem=recv_sem.at[slot],
                device_id=meets(*order[later]),
                device_id_type=pl.DeviceIdType.MESH,
            )
            copy.start()
            sent.append(copy)
            waiting.append((later, copy, mask + [order[later]], part, order))

    pass_on([], 0, 0, outer + [last])
    pass_on([], 0, 1, outer[::-1] + [last])
    own = pltpu.make_async_copy(x_ref, o_ref.at[group_at([])], own_sem)
    own.start()
    while waiting:
        first = min(range(len(waiting)), key=lambda at: waiting[at][0])
        stage, copy, mask, part, order = waiting.pop(first)
        copy.wait_recv()
        pass_on(mask, stage + 1, part, order)
    for copy in sent:
        copy.wait_send()
    own.wait()


def gather_groups(value):
    count = lax.axis_size("section") * lax.axis_size("dp")
    size = count * value.size * value.dtype.itemsize
    if size > KERNEL_BYTES:
        return lax.all_gather(value, ("section", "dp"), axis=0, tiled=True)
    slots = 2 * (count - 1)
    got = vmem_call(
        gather_kernel,
        jax.ShapeDtypeStruct((count,) + value.shape, value.dtype),
        [
            pltpu.SemaphoreType.DMA((slots,)),
            pltpu.SemaphoreType.DMA((slots,)),
            pltpu.SemaphoreType.DMA,
        ],
        size,
        4,
        value,
    )
    return got.reshape(-1, value.shape[1])


def scatter_kernel(x_ref, o_ref, held, taken, send_sem, recv_sem):
    outer, first = group_bits()
    greet(outer + [first])
    rows = x_ref.shape[1]
    half = x_ref.shape[2] // 2
    chunk = 32
    orders = ([first] + outer, [first] + outer[::-1])
    slots = iter(range(send_sem.shape[0]))
    masks = [[]]
    for bit in outer:
        masks = masks + [mask + [bit] for mask in masks]
    place_of = {frozenset(mask): at for at, mask in enumerate(masks)}
    base = len(masks)
    live = {}

    def send(part, stage):
        cols = pl.ds(part * half, half)
        bit = orders[part][stage]
        kept = orders[part][stage + 1 :]
        copies = []
        for mask in [m for m in masks if set(m) <= set(kept)]:
            if stage == 0:
                source = x_ref.at[group_at(mask + [bit]), :, cols]
            else:
                source = held.at[place_of[frozenset(mask + [bit])], :, cols]
            landing = 2 * base - 2 ** (len(kept) + 1) + [
                m for m in masks if set(m) <= set(kept)
            ].index(mask)
            slot = next(slots)
            copy = pltpu.make_async_remote_copy(
                src_ref=source,
                dst_ref=taken.at[landing, :, cols],
                send_sem=send_sem.at[slot],
                recv_sem=recv_sem.at[slot],
                device_id=meets(*bit),
                device_id_type=pl.DeviceIdType.MESH,
            )
            copy.start()
            copies.append((copy, mask, landing))
        live[part, stage] = copies

    def add(part, stage):
        cols = pl.ds(part * half, half)
        final = stage + 1 == len(orders[part])
        following = None if final else orders[part][stage + 1]
        copies = live[part, stage]
        for copy, mask, landing in sorted(copies, key=lambda c: following not in c[1]):
            copy.wait_recv()
            at = place_of[frozenset(mask)]
            spot = group_at(mask)

            @pl.loop(0, rows // chunk)
            def _(step):
                span = pl.ds(step * chunk, chunk)
                mine = x_ref[spot, span, cols] if stage == 0 else held[at, span, cols]
                total = mine.astype(jnp.float32) + taken[landing, span, cols].astype(jnp.float32)
                if final:
                    o_ref[span, cols] = total
                else:
                    held[at, span, cols] = total.astype(held.dtype)

    send(0, 0)
    send(1, 0)
    for stage in range(len(orders[0])):
        for part in (0, 1):
            add(part, stage)
            if stage + 1 < len(orders[0]):
                send(part, stage + 1)
    for copies in live.values():
        for copy, _, _ in copies:
            copy.wait_send()


def sum_scatter_groups(value):
    count = lax.axis_size("section") * lax.axis_size("dp")
    size = value.size * value.dtype.itemsize
    if size > KERNEL_BYTES:
        return lax.psum_scatter(value, ("section", "dp"), scatter_dimension=0, tiled=True)
    rows, cols = value.shape[0] // count, value.shape[1]
    slots = 2 * (count - 1)
    return vmem_call(
        scatter_kernel,
        jax.ShapeDtypeStruct((rows, cols), jnp.float32),
        [
            pltpu.VMEM((count // 2, rows, cols), value.dtype),
            pltpu.VMEM((count - 1, rows, cols), value.dtype),
            pltpu.SemaphoreType.DMA((slots,)),
            pltpu.SemaphoreType.DMA((slots,)),
        ],
        size,
        5,
        value.reshape(count, rows, cols),
    )


def per_device(
    patches,
    patch_counts,
    dest_rows,
    qkv_weight,
    out_weight,
    attn_gain,
    merge_gain,
    fc1_weight,
    fc1_bias,
    fc2_weight,
    fc2_bias,
    text_embeds,
    section_hidden,
    llm_gain,
):
    width = patches.shape[1]
    tile_total = patch_counts.shape[0]
    block_rows = patches.shape[0] // tile_total
    merged_rows = patches.shape[0] // 4
    local_cols = qkv_weight.shape[2]
    local_heads = local_cols // HEAD_DIM
    feature_cols = text_embeds.shape[1]
    seq_rows = text_embeds.shape[0]
    section_count = lax.axis_size("section")
    group_count = section_count * lax.axis_size("dp")
    run_cap = max(2, merged_rows // group_count)
    run_total = merged_rows // run_cap
    run_target = dest_rows.reshape(run_total, run_cap)[:, 0] // seq_rows
    takes = jnp.arange(group_count, dtype=jnp.int32)[:, None] == run_target[None, :]
    slot_in_tile = jnp.arange(merged_rows, dtype=jnp.int32) % (block_rows // 4)
    tile_counts = jnp.repeat(patch_counts, block_rows // 4, total_repeat_length=merged_rows)
    live = slot_in_tile * 4 < tile_counts
    place = jnp.where(live, dest_rows % seq_rows - seq_rows, 0).reshape(run_total, run_cap)
    send_place = jnp.sum(jnp.where(takes[:, :, None], place[None], 0), axis=1) + seq_rows
    got_place = lax.all_to_all(send_place, ("section", "dp"), split_axis=0, concat_axis=0, tiled=True)
    incoming = from_behind(section_hidden, "section", 1)
    normed_in = layer_norm(patches, attn_gain).astype(jnp.bfloat16)
    projections = jnp.dot(
        normed_in, qkv_weight.reshape(width, 3 * local_cols), preferred_element_type=jnp.float32
    ).astype(jnp.bfloat16)
    projections = projections.reshape(tile_total, block_rows, 3, local_heads, HEAD_DIM)
    query_part = projections[:, :, 0]
    key_part = projections[:, :, 1]
    value_part = projections[:, :, 2]
    scores = jnp.einsum(
        "tqhd,tkhd->thqk", query_part, key_part, preferred_element_type=jnp.float32
    ) * HEAD_DIM ** (-0.5)
    key_live = (
        jnp.arange(block_rows, dtype=jnp.int32)[None, None, None, :]
        < patch_counts[:, None, None, None]
    )
    scores = jnp.where(key_live, scores, -1e30)
    weights = jax.nn.softmax(scores, axis=-1).astype(jnp.bfloat16)
    attended = jnp.einsum(
        "thqk,tkhd->tqhd", weights, value_part, preferred_element_type=jnp.float32
    ).astype(jnp.bfloat16)
    attended = attended.reshape(patches.shape[0], local_cols)
    lane_source = jnp.arange(run_total, dtype=jnp.int32)[None, :] * run_cap
    run_source = jnp.sum(jnp.where(takes, lane_source, 0), axis=1)
    row_source = (
        run_source[:, None] + jnp.arange(run_cap, dtype=jnp.int32)[None, :]
    ).reshape(-1) * 4
    slots_at = jnp.arange(patches.shape[0], dtype=jnp.int32)
    patch_at = jnp.arange(4, dtype=jnp.int32)
    order = (
        (row_source[None, :] + patch_at[:, None]).reshape(-1)[:, None] == slots_at[None, :]
    ).astype(jnp.bfloat16)
    own_order = (
        (row_source + lax.axis_index("mp"))[:, None] == slots_at[None, :]
    ).astype(jnp.bfloat16)
    ordered = jnp.dot(order, attended, preferred_element_type=jnp.float32).astype(jnp.bfloat16)
    own_patch = jnp.dot(own_order, patches, preferred_element_type=jnp.float32)
    partial_proj = jnp.dot(ordered, out_weight, preferred_element_type=jnp.float32)
    own_proj = sum_scatter_mp(
        partial_proj.astype(jnp.bfloat16).reshape(4, group_count * run_cap, width), 0
    )
    block_out = (own_patch + own_proj).astype(jnp.bfloat16)
    merge_part = layer_norm(block_out, merge_gain).astype(jnp.bfloat16)
    slot_rows = group_count * run_cap
    gathered = gather_groups(merge_part)
    gathered = (
        gathered.reshape(group_count, group_count, run_cap, width)
        .transpose(1, 0, 2, 3)
        .reshape(group_count * slot_rows, width)
    )
    first_partial = jnp.dot(gathered, fc1_weight, preferred_element_type=jnp.float32)
    mp_count = lax.axis_size("mp")
    first_total = sum_scatter_mp(
        first_partial.astype(jnp.bfloat16).reshape(mp_count, -1, fc1_weight.shape[1]),
        1,
    )
    hidden_part = jax.nn.gelu(
        first_total + fc1_bias.astype(jnp.float32), approximate=False
    ).astype(jnp.bfloat16)
    hidden = gather_mp(hidden_part)
    second_partial = jnp.dot(hidden, fc2_weight, preferred_element_type=jnp.float32)
    embed_total = sum_scatter_groups(second_partial.astype(jnp.bfloat16)).astype(jnp.float32)
    image_embeds = (embed_total + fc2_bias.astype(jnp.float32)).astype(jnp.bfloat16)
    hits = got_place.reshape(1, -1) == jnp.arange(seq_rows, dtype=jnp.int32)[:, None]
    placed = jnp.dot(
        hits.astype(jnp.bfloat16), image_embeds, preferred_element_type=jnp.float32
    ).astype(jnp.bfloat16)
    sequence_embeds = jnp.where(jnp.any(hits, axis=1)[:, None], placed, text_embeds)
    entering = jnp.where(lax.axis_index("section") == 0, sequence_embeds, incoming).astype(
        jnp.float32
    )
    row_total = total_mp(jnp.sum(entering * entering, axis=1))
    layer_inputs = (
        entering * lax.rsqrt(row_total / HID + llm_eps)[:, None] * llm_gain.astype(jnp.float32)
    ).astype(jnp.bfloat16)
    return (sequence_embeds, layer_inputs)


def solution(mesh):
    in_specs = (
        P(("section", "dp"), None),
        P(("section", "dp")),
        P(("section", "dp")),
        P(None, None, "mp"),
        P("mp", None),
        P(),
        P(),
        P("mp", ("section", "dp")),
        P(("section", "dp")),
        P(("section", "dp"), "mp"),
        P("mp"),
        P(("section", "dp"), "mp"),
        P(("section", "dp"), "mp"),
        P("mp"),
    )
    out_specs = (P(("section", "dp"), "mp"), P(("section", "dp"), "mp"))
    return jax.shard_map(
        per_device, mesh=mesh, in_specs=in_specs, out_specs=out_specs, check_vma=False
    )
```

profile of v0, /device:TPU:0, one launch (start us, length us, event | category | flops | bytes accessed | tf_op | source)
XLA Modules:
  0.0 221.2 jit_solution(15574821456396241994)
XLA Ops:
  0.6 0.0 copy-start
  0.6 0.0 copy-start.2
  0.7 0.9 reshape.244
  1.5 0.1 slice_reduce_fusion
  1.7 1.3 fusion.44
  3.0 2.0 compare_select_fusion.2
  5.0 0.1 broadcast_in_dim.58
  5.1 0.1 select_reduce_fusion
  5.2 0.6 broadcast_add_fusion
  5.7 5.2 %all-to-all-start = ((s32[8,1,16]{2,1,0:T(1,128)}), s32[8,1,16]{2,1,0:T(1,128)}, u32[]{:S(2)}, u32[]{:S(2)}) async-start(s32[8,1,16]{2,1,0:T(1,128)} %bitcast.3), calls=%async_computation | async-start | bytes 8192 | tf_op jit(solution)/shard_map/all_to_all | solution.py:408
  10.9 0.0 copy-start.1
  10.9 5.4 %collective-permute-start = (bf16[512,2048]{1,0:T(8,128)(2,1)}, bf16[512,2048]{1,0:T(8,128)(2,1)}, u32[]{:S(2)}, u32[]{:S(2)}) collective-permute-start(bf16[512,2048]{1,0:T(8,128)(2,1)} %param.28), channel_id=1, source_target_pairs={{0,16},{1,17},{2,18},{3,19},{4,20},{5,21},{6,22},{7,23},{8,24},{9,... | collective-permute-start | bytes 6291464 | tf_op jit(solution)/shard_map/ppermute | solution.py:22
  16.3 0.7 iota_compare_fusion.8
  17.1 1.6 convert_reduce_fusion
  18.6 0.0 copy-done.1
  18.6 0.5 fusion.7
  19.1 0.0 copy-done.2
  19.1 4.3 %convolution_convert_fusion.4 = bf16[512,960]{0,1:T(8,128)(2,1)} fusion(bf16[1280,960]{0,1:T(8,128)(2,1)} %bitcast.65, bf16[512,1280]{1,0:T(8,128)(2,1)S(1)} %copy-done.1, f32[1280]{0:T(1024)S(1)} %convert_element_type.79, f32[512]{0:T(512)S(1)} %add_rsqrt_fusion, f32[512]{0:T(512)S(1)} %broadcast_multiply_fusion), kind=kOutput, calls=%fused_computation.28 | convolution fusion | flops 1262059520 | bytes 4760576 | tf_op jit(solution)/shard_map/dot_general | solution.py:411
  23.4 3.3 %reshape.246 = bf16[2,256,3,4,80]{1,0,4,3,2:T(2,128)(2,1)} reshape(bf16[512,960]{0,1:T(8,128)(2,1)} %convolution_convert_fusion.4) | data formatting | bytes 1966080 | tf_op jit(solution)/shard_map/reshape | solution.py:414
  26.7 2.7 %fusion.43 = (bf16[2,256,1,4,80]{1,0,4,3,2:T(2,128)(2,1)S(1)}, bf16[2,256,1,4,80]{1,0,4,3,2:T(2,128)(2,1)S(1)}, bf16[2,256,1,4,80]{1,0,4,3,2:T(2,128)(2,1)}) fusion(bf16[2,256,3,4,80]{1,0,4,3,2:T(2,128)(2,1)} %reshape.246), kind=kLoop, calls=%fused_computation.101 | loop fusion | bytes 1966080 | tf_op jit(solution)/shard_map/slice | solution.py:417
  29.4 3.2 %fusion.45 = (f32[2,4,256]{2,1,0:T(4,128)S(1)}, f32[2,4,256,256]{2,3,1,0:T(8,128)}) fusion(pred[2,256]{1,0:T(4,128)(4,1)S(1)} %iota_compare_fusion.8, bf16[2,256,1,4,80]{1,0,4,3,2:T(2,128)(2,1)} %get-tuple-element.16, bf16[2,256,1,4,80]{1,0,4,3,2:T(2,128)(2,1)S(1)} %get-tuple-element.15), kind=kOutput, calls=%fused_computation.103 | convolution fusion | flops 85983488 | bytes 2761216 | tf_op jit(solution)/shard_map/sub | solution.py:426
  32.6 1.9 fusion.17
  34.5 0.3 copy.38
  34.8 0.1 select_reduce_fusion.1
  35.0 0.1 add_multiply_fusion
  35.0 0.1 mul.106
  35.1 3.5 %convolution_convert_fusion.2 = bf16[512,1280]{1,0:T(8,128)(2,1)} fusion(bf16[320,1280]{1,0:T(8,128)(2,1)} %param.20, bf16[512,320]{0,1:T(8,128)(2,1)S(1)} %bitcast.64, s32[512]{0:T(512)S(1)} %add_bitcast_fusion), kind=kOutput, calls=%fused_computation.12 | convolution fusion | flops 588283904 | bytes 2459648 | tf_op jit(solution)/shard_map/dot_general | solution.py:446
  38.6 28.2 %shard_map.149 = bf16[4,128,1280]{2,1,0:T(8,128)(2,1)} custom-call(bf16[4,128,1280]{2,1,0:T(8,128)(2,1)} %bitcast.67), custom_call_target="tpu_custom_call" | custom-call | flops 26214400000 | bytes 2621440 | tf_op jit(solution)/shard_map/pallas_call | solution.py:37
  66.8 1.6 convert_reduce_fusion.2
  68.4 0.0 copy-start.3
  68.4 1.8 fusion.46
  70.2 0.2 multiply_reduce_fusion
  70.4 0.0 copy-done.3
  70.5 0.9 multiply_convert_fusion.x_ref
  71.4 19.1 %shard_map.150 = bf16[8,128,1280]{2,1,0:T(8,128)(2,1)} custom-call(bf16[128,1280]{1,0:T(8,128)(2,1)} %multiply_convert_fusion.x_ref), custom_call_target="tpu_custom_call" | custom-call | flops 52428800000 | bytes 5242880 | tf_op jit(solution)/shard_map/pallas_call | solution.py:37
  90.5 0.0 copy-start.7
  90.5 2.1 copy.39
  92.6 0.1 copy-done.7
  92.7 3.3 %convolution_convert_fusion.3 = bf16[1024,640]{1,0:T(8,128)(2,1)} fusion(bf16[1024,1280]{1,0:T(8,128)(2,1)S(1)} %bitcast.62, bf16[1280,640]{1,0:T(8,128)(2,1)S(1)} %copy-done.7), kind=kOutput, calls=%fused_computation.27 | convolution fusion | flops 1678376960 | bytes 5570560 | tf_op jit(solution)/shard_map/dot_general | solution.py:459
  96.0 0.0 copy-start.6
  96.0 34.0 %shard_map.151 = bf16[4,256,640]{2,1,0:T(8,128)(2,1)} custom-call(bf16[4,256,640]{2,1,0:T(8,128)(2,1)} %bitcast.68), custom_call_target="tpu_custom_call" | custom-call | flops 26214400000 | bytes 2621440 | tf_op jit(solution)/shard_map/pallas_call | solution.py:37
  130.0 1.6 convert_reduce_fusion.1
  131.6 0.0 copy-done.6
  131.6 2.2 fusion.23.x_ref
  133.7 32.9 %shard_map.152 = bf16[4,256,640]{2,1,0:T(8,128)(2,1)} custom-call(bf16[256,640]{1,0:T(8,128)(2,1)} %fusion.23.x_ref), custom_call_target="tpu_custom_call" | custom-call | flops 26214400000 | bytes 2621440 | tf_op jit(solution)/shard_map/pallas_call | solution.py:37
  166.6 0.0 copy-done
  166.6 6.3 %convolution_convert_fusion = bf16[1024,2048]{1,0:T(8,128)(2,1)} fusion(bf16[1024,640]{1,0:T(8,128)(2,1)} %bitcast.69, bf16[640,2048]{1,0:T(8,128)(2,1)S(1)} %copy-done), kind=kOutput, calls=%fused_computation.6 | convolution fusion | flops 2686451712 | bytes 8126464 | tf_op jit(solution)/shard_map/dot_general | solution.py:469
  172.9 0.0 copy-start.4
  172.9 0.0 copy-start.5
  172.9 29.5 %shard_map.153 = f32[128,2048]{1,0:T(8,128)} custom-call(bf16[8,128,2048]{2,1,0:T(8,128)(2,1)} %bitcast.66), custom_call_target="tpu_custom_call" | custom-call | flops 83886080000 | bytes 8388608 | tf_op jit(solution)/shard_map/pallas_call | solution.py:37
  202.5 0.0 copy-done.4
  202.5 0.0 copy-done.5
  202.5 0.0 all-to-all-done
  202.5 0.5 broadcast.253
  203.0 1.3 reduce.7
  204.4 0.1 eq.67
  204.5 0.2 fusion.35
  204.6 0.0 collective-permute-done
  204.6 5.0 %fusion.1 = (f32[512]{0:T(512)}, bf16[512,2048]{1,0:T(8,128)(2,1)}) fusion(bf16[512,2048]{1,0:T(8,128)(2,1)} %collective-permute-done, pred[]{:T(512)S(6)} %eq.77, bf16[512,2048]{1,0:T(8,128)(2,1)} %param.27, f32[128,2048]{1,0:T(8,128)} %shard_map.153, f32[2048]{0:T(1024)S(1)} %convert_element_type.97, s32[128]{0:T(128)S(1)} %eq.67, ...), kind=kOutput, calls=%fused_computation.3 | convolution fusion | flops 275316224 | bytes 7351297 | tf_op jit(solution)/shard_map/dot_general | solution.py:473
  209.6 6.7 %shard_map.154 = f32[4,4,128]{2,1,0:T(4,128)} custom-call(f32[4,128]{1,0:T(4,128)} %bitcast.70), custom_call_target="tpu_custom_call" | custom-call | flops 163840000 | bytes 16384 | tf_op jit(solution)/shard_map/pallas_call | solution.py:37
  216.4 0.7 reduce_sum.109
  217.1 4.1 %fusion.3 = bf16[512,2048]{1,0:T(8,128)(2,1)} fusion(f32[2048]{0:T(1024)S(1)} %convert_element_type.101, f32[512]{0:T(512)S(1)} %rsqrt_bitcast_fusion, bf16[512,2048]{1,0:T(8,128)(2,1)} %get-tuple-element.24, bf16[512,2048]{1,0:T(8,128)(2,1)} %collective-permute-done, pred[]{:T(512)S(6)} %eq.77), kind=kLoop, calls=%fused_computation.5 | loop fusion | flops 5242880 | bytes 6301697 | tf_op jit(solution)/shard_map/convert_element_type | solution.py:483
  (15 shorter events, 0.1 us)
Async XLA Ops:
  0.6 166.0 %copy-start = (bf16[640,2048]{1,0:T(8,128)(2,1)S(1)}, bf16[640,2048]{1,0:T(8,128)(2,1)}, u32[]{:S(2)}) copy-start(bf16[640,2048]{1,0:T(8,128)(2,1)} %param.25) | copy-start | bytes 7864324
  0.6 18.5 %copy-start.2 = (bf16[1280]{0:T(1024)(128)(2,1)S(1)}, bf16[1280]{0:T(1024)(128)(2,1)}, u32[]{:S(2)}) copy-start(bf16[1280]{0:T(1024)(128)(2,1)} %param.21) | copy-start | bytes 7684
  5.7 196.8 %all-to-all-start = ((s32[8,1,16]{2,1,0:T(1,128)}), s32[8,1,16]{2,1,0:T(1,128)}, u32[]{:S(2)}, u32[]{:S(2)}) async-start(s32[8,1,16]{2,1,0:T(1,128)} %bitcast.3), calls=%async_computation | async-start | bytes 8192 | tf_op jit(solution)/shard_map/all_to_all | solution.py:408
  10.9 7.7 %copy-start.1 = (bf16[512,1280]{1,0:T(8,128)(2,1)S(1)}, bf16[512,1280]{1,0:T(8,128)(2,1)}, u32[]{:S(2)}) copy-start(bf16[512,1280]{1,0:T(8,128)(2,1)} %param.16) | copy-start | bytes 3932164
  10.9 193.7 %collective-permute-start = (bf16[512,2048]{1,0:T(8,128)(2,1)}, bf16[512,2048]{1,0:T(8,128)(2,1)}, u32[]{:S(2)}, u32[]{:S(2)}) collective-permute-start(bf16[512,2048]{1,0:T(8,128)(2,1)} %param.28), channel_id=1, source_target_pairs={{0,16},{1,17},{2,18},{3,19},{4,20},{5,21},{6,22},{7,23},{8,24},{9,... | collective-permute-start | bytes 6291464 | tf_op jit(solution)/shard_map/ppermute | solution.py:22
  68.4 2.0 copy-start.3
  90.5 2.2 %copy-start.7 = (bf16[1280,640]{1,0:T(8,128)(2,1)S(1)}, bf16[1280,640]{1,0:T(8,128)(2,1)}, u32[]{:S(2)}) copy-start(bf16[1280,640]{1,0:T(8,128)(2,1)} %param.23) | copy-start | bytes 4915204
  96.0 35.6 %copy-start.6 = (bf16[640]{0:T(1024)(128)(2,1)S(1)}, bf16[640]{0:T(1024)(128)(2,1)}, u32[]{:S(2)}) copy-start(bf16[640]{0:T(1024)(128)(2,1)} %param.24) | copy-start | bytes 3844
  172.9 29.5 %copy-start.4 = (bf16[2048]{0:T(1024)(128)(2,1)S(1)}, bf16[2048]{0:T(1024)(128)(2,1)}, u32[]{:S(2)}) copy-start(bf16[2048]{0:T(1024)(128)(2,1)} %param.26) | copy-start | bytes 12292
  172.9 29.6 %copy-start.5 = (bf16[2048]{0:T(1024)(128)(2,1)S(1)}, bf16[2048]{0:T(1024)(128)(2,1)}, u32[]{:S(2)}) copy-start(bf16[2048]{0:T(1024)(128)(2,1)} %param.29) | copy-start | bytes 12292
where the time goes:
time: 222 us; the launch traced here: 221 us
  Pallas kernels  150 us (68%)
  matrix products  29.1 us (13%)
  other arithmetic  18.4 us (8%)
  local copies, waits for them, and re-layouts  11.6 us (5%)
  starting transfers between devices  10.6 us (5%)
    pallas_call x6, Pallas kernels, vmem_call(): pl.pallas_call(kernel, out_shape=out, in_specs=[pl.BlockSpec(memory_space...  150 us
    dot_general x1, matrix products, per_device(): jnp.dot(hidden, fc2_weight, preferred_element_type=jnp.float32)  6.29 us
    ppermute x1, starting transfers between devices, from_behind(): lax.ppermute(value, axis, [(source, source + steps) for source in range(f...  5.38 us
    all_to_all x1, starting transfers between devices, per_device(): lax.all_to_all(send_place, ('section', 'dp'), split_axis=0, concat_axis=0...  5.2 us
    dot_general x1, matrix products, per_device(): jnp.dot(hits.astype(jnp.bfloat16), image_embeds, preferred_element_type=j...  4.97 us
  transfers between devices with their start and end apart: 2, of which 0 were waited for; matrix products, arithmetic and copies ran while one was open for 20% of the time, Pallas kernels for 65%

commit v1 on v0

--- a/solution.py
+++ b/solution.py
@@ -370,7 +370,7 @@
     )
 
 
-def per_device(
+def plain_per_device(
     patches,
     patch_counts,
     dest_rows,
@@ -484,6 +484,667 @@
     return (sequence_embeds, layer_inputs)
 
 
+LAG = 2
+FC2_COLS = 512
+HALF_ROOT = 0.5**0.5
+
+
+def remote(src, dst, send_sem, recv_sem, device):
+    return pltpu.make_async_remote_copy(
+        src_ref=src,
+        dst_ref=dst,
+        send_sem=send_sem,
+        recv_sem=recv_sem,
+        device_id=device,
+        device_id_type=pl.DeviceIdType.MESH,
+    )
+
+
+def group_device(group):
+    per_section = lax.axis_size("dp")
+    return {"section": group // per_section, "dp": lax.rem(group, per_section)}
+
+
+def tell(device):
+    pl.semaphore_signal(
+        pltpu.get_barrier_semaphore(),
+        inc=1,
+        device_id=device,
+        device_id_type=pl.DeviceIdType.MESH,
+    )
+
+
+def merger_kernel(
+    x_ref,
+    place_ref,
+    sums_ref,
+    w1_ref,
+    b1_ref,
+    w2_ref,
+    b2_ref,
+    img_ref,
+    spot_ref,
+    base_ref,
+    total_ref,
+    rows,
+    part,
+    before,
+    after,
+    right_out,
+    left_out,
+    hidden,
+    give,
+    take,
+    keep,
+    x_out,
+    x_in,
+    y_out,
+    y_in,
+    squares,
+    spots,
+    sums,
+    base_out,
+    base_in,
+    totals,
+    row_send,
+    row_recv,
+    pair_recv,
+    right_send,
+    right_recv,
+    left_send,
+    left_recv,
+    give_send,
+    give_recv,
+    x_send,
+    x_recv,
+    y_send,
+    y_recv,
+    spot_send,
+    spot_recv,
+    sum_send,
+    sum_recv,
+    base_send,
+    base_recv,
+    total_send,
+    total_recv,
+):
+    groups = lax.axis_size("section") * lax.axis_size("dp")
+    sections = lax.axis_size("section")
+    line = lax.axis_size("mp")
+    me = lax.axis_index("mp")
+    section = lax.axis_index("section")
+    dp = lax.axis_index("dp")
+    core = lax.rem(dp, 2)
+    column = dp // 2
+    wide = lax.axis_size("dp") // 2
+    group = section * lax.axis_size("dp") + dp
+    chips = groups // 2
+    pair = {"dp": flip(dp, 1)}
+    over_x = {"dp": flip(dp, 2)}
+    over_y = {"section": flip(section, 1)}
+    quarters = 4
+    pieces = chips * quarters
+    take_rows = rows.shape[2] // 2
+    lag_right = me * LAG
+    lag_left = (line - 1 - me) * LAG
+    lag_total = (line - 1) * LAG
+
+    for step in range(1, groups):
+        tell(group_device(lax.rem(group + step, groups)))
+    for step in range(1, line):
+        tell({"mp": lax.rem(me + step, line)})
+    pl.semaphore_wait(pltpu.get_barrier_semaphore(), groups + line - 2)
+
+    def chip_of(quarter):
+        there_x = lax.rem(quarter // 2 + column, 2)
+        there_y = lax.rem(lax.rem(quarter, 2) + section, 2)
+        return there_y * wide + there_x
+
+    def group_of(quarter, at_core):
+        return chip_of(quarter) * 2 + at_core
+
+    def own_sends(chunk):
+        return (
+            remote(x_ref.at[chunk], rows.at[group, chunk], row_send.at[chunk, 0], row_recv.at[chunk, 1], over_y),
+            remote(x_ref.at[chunk], rows.at[group, chunk], row_send.at[chunk, 1], row_recv.at[chunk, 2], over_x),
+            remote(x_ref.at[chunk], rows.at[group, chunk], row_send.at[chunk, 2], pair_recv.at[chunk, 0], pair),
+        )
+
+    def forward_x(chunk):
+        spot = rows.at[group_of(1, core), chunk]
+        return remote(spot, spot, row_send.at[chunk, 3], row_recv.at[chunk, 3], over_x)
+
+    def forward_pair(chunk, quarter):
+        spot = rows.at[group_of(quarter, core), chunk]
+        return remote(
+            spot, spot, row_send.at[chunk, 3 + quarter], pair_recv.at[chunk, quarter], pair
+        )
+
+    for copy in own_sends(0):
+        copy.start()
+
+    place_copies = []
+    for step in range(1, groups):
+        peer = lax.rem(group + step, groups)
+        copy = remote(
+            place_ref.at[peer], spots.at[step], spot_send.at[step - 1], spot_recv.at[step - 1], group_device(peer)
+        )
+        copy.start()
+        place_copies.append(copy)
+    sum_copies = []
+    for step in range(1, line):
+        peer = lax.rem(me + step, line)
+        copy = remote(sums_ref, sums.at[step], sum_send.at[step - 1], sum_recv.at[step - 1], {"mp": peer})
+        copy.start()
+        sum_copies.append(copy)
+    spots[0] = place_ref[group]
+    sums[0] = sums_ref[...]
+    rows[group] = x_ref[...]
+
+    def send_right(piece):
+        return remote(
+            right_out.at[piece], before.at[piece], right_send.at[piece], right_recv.at[piece], {"mp": me + 1}
+        )
+
+    def send_left(piece):
+        return remote(
+            left_out.at[piece], after.at[piece], left_send.at[piece], left_recv.at[piece], {"mp": me - 1}
+        )
+
+    def send_give(chunk):
+        return remote(give.at[chunk], take.at[chunk], give_send.at[chunk], give_recv.at[chunk], pair)
+
+    parts = x_send.shape[1]
+    span = keep.shape[1] // parts
+
+    def send_x(chunk, at):
+        cut = pl.ds(at * span, span)
+        return remote(
+            x_out.at[chunk, cut], x_in.at[chunk, cut], x_send.at[chunk, at], x_recv.at[chunk, at], over_x
+        )
+
+    def send_y(at):
+        cut = pl.ds(at * span, span)
+        return remote(y_out.at[cut], y_in.at[cut], y_send.at[at], y_recv.at[at], over_y)
+
+    def settle(chunk):
+        send_give(chunk).wait_recv()
+        mine = lax.rem(chunk, wide) == column
+
+        @pl.when(mine)
+        def _():
+            @pl.loop(0, parts)
+            def _(at):
+                cut = pl.ds(at * span, span)
+                keep[chunk, cut] = keep[chunk, cut] + take[chunk, cut].astype(jnp.float32)
+
+        @pl.when(jnp.logical_not(mine))
+        def _():
+            @pl.loop(0, parts)
+            def _(at):
+                cut = pl.ds(at * span, span)
+                x_out[chunk, cut] = (
+                    keep[chunk, cut] + take[chunk, cut].astype(jnp.float32)
+                ).astype(x_out.dtype)
+                send_x(chunk, at).start()
+
+    def stage(i, carry):
+        @pl.when(i < pieces)
+        def _():
+            chunk = i // quarters
+            quarter = lax.rem(i, quarters)
+
+            @pl.when(quarter == 1)
+            def _():
+                remote(
+                    x_ref.at[chunk], rows.at[group_of(1, core), chunk], row_send.at[chunk, 0], row_recv.at[chunk, 1], over_y
+                ).wait_recv()
+                forward_x(chunk).start()
+                forward_pair(chunk, 1).start()
+
+                @pl.when(chunk + 1 < chips)
+                def _():
+                    for copy in own_sends(chunk + 1):
+                        copy.start()
+
+            @pl.when(quarter > 1)
+            def _():
+                remote(
+                    x_ref.at[chunk], rows.at[group_of(quarter, core), chunk], row_send.at[chunk, 1], row_recv.at[chunk, quarter], over_x
+                ).wait_recv()
+                forward_pair(chunk, quarter).start()
+
+        at_dot = i - 1
+
+        @pl.when(jnp.logical_and(at_dot >= 0, at_dot < pieces))
+        def _():
+            chunk = at_dot // quarters
+            quarter = lax.rem(at_dot, quarters)
+            spot = rows.at[group_of(quarter, 1 - core), chunk]
+            remote(x_ref.at[chunk], spot, row_send.at[chunk, 2], pair_recv.at[chunk, quarter], pair).wait_recv()
+            lhs = rows[pl.ds(chip_of(quarter) * 2, 2), chunk]
+            part[at_dot] = jnp.dot(
+                lhs.reshape(part.shape[1], lhs.shape[2]), w1_ref[...], preferred_element_type=jnp.float32
+            )
+
+        at_right = i - 1 - lag_right
+
+        @pl.when(jnp.logical_and(me < line - 1, jnp.logical_and(at_right >= 0, at_right < pieces)))
+        def _():
+            @pl.when(me == 0)
+            def _():
+                right_out[at_right] = part[at_right].astype(right_out.dtype)
+
+            @pl.when(me > 0)
+            def _():
+                send_right(at_right).wait_recv()
+                right_out[at_right] = (
+                    part[at_right] + before[at_right].astype(jnp.float32)
+                ).astype(right_out.dtype)
+
+            send_right(at_right).start()
+
+        at_left = i - 1 - lag_left
+
+        @pl.when(jnp.logical_and(me > 0, jnp.logical_and(at_left >= 0, at_left < pieces)))
+        def _():
+            @pl.when(me == line - 1)
+            def _():
+                left_out[at_left] = part[at_left].astype(left_out.dtype)
+
+            @pl.when(me < line - 1)
+            def _():
+                send_left(at_left).wait_recv()
+                left_out[at_left] = (
+                    part[at_left] + after[at_left].astype(jnp.float32)
+                ).astype(left_out.dtype)
+
+            send_left(at_left).start()
+
+        at_total = i - 1 - lag_total
+
+        @pl.when(at_total >= 0)
+        def _():
+            chunk = at_total // quarters
+            quarter = lax.rem(at_total, quarters)
+
+            @pl.when(jnp.logical_and(quarter == 0, chunk > 0))
+            def _():
+                settle(chunk - 1)
+
+            @pl.when(me == line - 1)
+            def _():
+                send_right(at_total).wait_recv()
+
+            @pl.when(me == 0)
+            def _():
+                send_left(at_total).wait_recv()
+
+            @pl.when(me > 0)
+            def _():
+                part[at_total] = part[at_total] + before[at_total].astype(jnp.float32)
+
+            @pl.when(me < line - 1)
+            def _():
+                part[at_total] = part[at_total] + after[at_total].astype(jnp.float32)
+
+            value = part[at_total] + b1_ref[...]
+            value = 0.5 * value * (1.0 + lax.erf(value * HALF_ROOT))
+            hidden[chunk, chip_of(quarter)] = value.astype(hidden.dtype).reshape(hidden.shape[2:])
+
+            @pl.when(quarter == quarters - 1)
+            def _():
+                for_pair = hidden[chunk, :, :, 1 - core].reshape(-1, hidden.shape[5])
+                for_me = hidden[chunk, :, :, core].reshape(-1, hidden.shape[5])
+                count = for_me.shape[0]
+                lhs = jnp.concatenate([for_pair, for_me], axis=0)
+
+                @pl.loop(0, w2_ref.shape[1] // FC2_COLS)
+                def _(at):
+                    cols = pl.ds(pl.multiple_of(at * FC2_COLS, FC2_COLS), FC2_COLS)
+                    result = jnp.dot(lhs, w2_ref[:, cols], preferred_element_type=jnp.float32)
+                    give[chunk, :, cols] = result[:count].astype(give.dtype)
+                    keep[chunk, :, cols] = result[count:]
+
+                send_give(chunk).start()
+
+        return carry
+
+    lax.fori_loop(0, pieces + 1 + lag_total, stage, 0)
+    settle(chips - 1)
+
+    for copy in sum_copies:
+        copy.wait_recv()
+    sum_rows = base_out.shape[0]
+    both = sums[0]
+    for step in range(1, line):
+        both = both + sums[step]
+    base_out[...] = both[sum_rows:]
+    base_ref[...] = both[:sum_rows]
+    send_base = remote(base_out, base_in, base_send, base_recv, {"section": section + 1})
+
+    @pl.when(section < sections - 1)
+    def _():
+        send_base.start()
+
+    spot_sum = spots[0]
+    for copy in place_copies:
+        copy.wait_recv()
+    for step in range(1, groups):
+        spot_sum = spot_sum + spots[step]
+    spot_ref[...] = spot_sum
+
+    @pl.when(section > 0)
+    def _():
+        send_base.wait_recv()
+        base_ref[...] = base_in[...]
+
+    own_chunk = section * wide + column
+    y_chunk = flip(section, 1) * wide + column
+
+    @pl.loop(0, parts)
+    def _(at):
+        cut = pl.ds(at * span, span)
+        send_x(y_chunk, at).wait_recv()
+        y_out[cut] = (keep[y_chunk, cut] + x_in[y_chunk, cut].astype(jnp.float32)).astype(y_out.dtype)
+        send_y(at).start()
+
+    @pl.loop(0, parts)
+    def _(at):
+        cut = pl.ds(at * span, span)
+        send_x(own_chunk, at).wait_recv()
+        send_y(at).wait_recv()
+        value = (
+            keep[own_chunk, cut]
+            + x_in[own_chunk, cut].astype(jnp.float32)
+            + y_in[cut].astype(jnp.float32)
+            + b2_ref[...]
+        ).astype(img_ref.dtype)
+        img_ref[cut] = value
+        value = value.astype(jnp.float32)
+        square = value * value
+        width = squares.shape[1]
+        folded = square[:, :width]
+        for at_col in range(1, square.shape[1] // width):
+            folded = folded + square[:, at_col * width : (at_col + 1) * width]
+        squares[cut] = folded
+
+    totals[0] = jnp.sum(squares[...].T, axis=0, keepdims=True)
+    total_copies = []
+    for step in range(1, line):
+        copy = remote(
+            totals.at[0], totals.at[step], total_send.at[step - 1], total_recv.at[step - 1], {"mp": lax.rem(me + step, line)}
+        )
+        copy.start()
+        total_copies.append(copy)
+
+    for chunk in range(chips):
+        for copy in own_sends(chunk):
+            copy.wait_send()
+        forward_x(chunk).wait_send()
+        for quarter in range(1, quarters):
+            forward_pair(chunk, quarter).wait_send()
+        send_give(chunk).wait_send()
+
+        @pl.when(chunk % wide != column)
+        def _():
+            for at in range(parts):
+                send_x(chunk, at).wait_send()
+
+    for at in range(parts):
+        send_y(at).wait_send()
+
+    @pl.when(me < line - 1)
+    def _():
+        @pl.loop(0, pieces)
+        def _(piece):
+            send_right(piece).wait_send()
+
+    @pl.when(me > 0)
+    def _():
+        @pl.loop(0, pieces)
+        def _(piece):
+            send_left(piece).wait_send()
+
+    for copy in place_copies + sum_copies:
+        copy.wait_send()
+
+    @pl.when(section < sections - 1)
+    def _():
+        send_base.wait_send()
+
+    row_total = totals[0]
+    for step, copy in enumerate(total_copies):
+        copy.wait()
+        row_total = row_total + totals[step + 1]
+    total_ref[...] = row_total
+
+
+def merger(rows, places, sums, w1, b1, w2, b2):
+    groups = lax.axis_size("section") * lax.axis_size("dp")
+    line = lax.axis_size("mp")
+    chips = groups // 2
+    chunk_rows = rows.shape[0] // chips
+    run = chunk_rows // 2
+    width = rows.shape[1]
+    units = w1.shape[1]
+    features = w2.shape[1]
+    pieces = chips * 4
+    piece_rows = 2 * chunk_rows
+    target_rows = groups * run
+    parts = 4
+    low = jnp.bfloat16
+    dma = pltpu.SemaphoreType.DMA
+    sum_rows = sums.shape[0] // 2
+    return pl.pallas_call(
+        merger_kernel,
+        out_shape=(
+            jax.ShapeDtypeStruct((target_rows, features), low),
+            jax.ShapeDtypeStruct(places.shape[1:], jnp.int32),
+            jax.ShapeDtypeStruct((sum_rows, sums.shape[1]), jnp.float32),
+            jax.ShapeDtypeStruct((1, target_rows), jnp.float32),
+        ),
+        in_specs=[pl.BlockSpec(memory_space=pltpu.VMEM)] * 7,
+        out_specs=[pl.BlockSpec(memory_space=pltpu.VMEM)] * 4,
+        scratch_shapes=[
+            pltpu.VMEM((groups, chips, chunk_rows, width), low),
+            pltpu.VMEM((pieces, piece_rows, units), jnp.float32),
+            pltpu.VMEM((pieces, piece_rows, units), low),
+            pltpu.VMEM((pieces, piece_rows, units), low),
+            pltpu.VMEM((pieces, piece_rows, units), low),
+            pltpu.VMEM((pieces, piece_rows, units), low),
+            pltpu.VMEM((chips, chips, 2, 2, run, units), low),
+            pltpu.VMEM((chips, target_rows, features), low),
+            pltpu.VMEM((chips, target_rows, features), low),
+            pltpu.VMEM((chips, target_rows, features), jnp.float32),
+            pltpu.VMEM((chips, target_rows, features), low),
+            pltpu.VMEM((chips, target_rows, features), low),
+            pltpu.VMEM((target_rows, features), low),
+            pltpu.VMEM((target_rows, features), low),
+            pltpu.VMEM((target_rows, 128), jnp.float32),
+            pltpu.VMEM(places.shape, jnp.int32),
+            pltpu.VMEM((line,) + sums.shape, jnp.float32),
+            pltpu.VMEM((sum_rows, sums.shape[1]), jnp.float32),
+            pltpu.VMEM((sum_rows, sums.shape[1]), jnp.float32),
+            pltpu.VMEM((line, 1, target_rows), jnp.float32),
+            dma((chips, 7)),
+            dma((chips, 4)),
+            dma((chips, 4)),
+            dma((pieces,)),
+            dma((pieces,)),
+            dma((pieces,)),
+            dma((pieces,)),
+            dma((chips,)),
+            dma((chips,)),
+            dma((chips, parts)),
+            dma((chips, parts)),
+            dma((parts,)),
+            dma((parts,)),
+            dma((groups - 1,)),
+            dma((groups - 1,)),
+            dma((line - 1,)),
+            dma((line - 1,)),
+            dma,
+            dma,
+            dma((line - 1,)),
+            dma((line - 1,)),
+        ],
+        cost_estimate=pl.CostEstimate(
+            flops=10**11, bytes_accessed=10**7, transcendentals=0
+        ),
+        compiler_params=pltpu.CompilerParams(
+            collective_id=6, has_side_effects=True, vmem_limit_bytes=VMEM_LIMIT
+        ),
+    )(rows.reshape(chips, chunk_rows, width), places, sums, w1, b1, w2, b2)
+
+
+def placing_kernel(text_ref, incoming_ref, img_ref, spot_ref, total_ref, base_ref, gain_ref, seq_ref, layer_ref):
+    height = text_ref.shape[0]
+    at_row = pl.program_id(0) * height + lax.broadcasted_iota(jnp.int32, (height, spot_ref.shape[1]), 0)
+    hits = spot_ref[...] == at_row
+    hit = jnp.max(hits.astype(jnp.float32), axis=1, keepdims=True) > 0.0
+    placed = jnp.dot(
+        hits.astype(jnp.bfloat16), img_ref[...], preferred_element_type=jnp.float32
+    ).astype(jnp.bfloat16)
+    sequence = jnp.where(hit, placed, text_ref[...])
+    seq_ref[...] = sequence
+    gain = gain_ref[...].astype(jnp.float32)
+    base = base_ref[...]
+
+    @pl.when(lax.axis_index("section") == 0)
+    def _():
+        total = jnp.sum(jnp.where(hits, total_ref[...], 0.0), axis=1, keepdims=True)
+        total = jnp.where(hit, total, base)
+        scale = lax.rsqrt(total / HID + llm_eps)
+        layer_ref[...] = (sequence.astype(jnp.float32) * scale * gain).astype(layer_ref.dtype)
+
+    @pl.when(lax.axis_index("section") > 0)
+    def _():
+        scale = lax.rsqrt(base / HID + llm_eps)
+        layer_ref[...] = (incoming_ref[...].astype(jnp.float32) * scale * gain).astype(layer_ref.dtype)
+
+
+def placing(text, incoming, img, spot, total, base, gain):
+    rows, features = text.shape
+    height = rows // 8
+    block = pl.BlockSpec((height, features), lambda i: (i, 0))
+
+    def whole(value):
+        return pl.BlockSpec(value.shape, lambda i: (0, 0))
+
+    return pl.pallas_call(
+        placing_kernel,
+        grid=(rows // height,),
+        out_shape=(jax.ShapeDtypeStruct(text.shape, text.dtype),) * 2,
+        in_specs=[
+            block,
+            block,
+            whole(img),
+            whole(spot),
+            whole(total),
+            pl.BlockSpec((height, 1), lambda i: (i, 0)),
+            whole(gain),
+        ],
+        out_specs=(block, block),
+        cost_estimate=pl.CostEstimate(flops=10**9, bytes_accessed=10**7, transcendentals=0),
+    )(text, incoming, img, spot, total, base, gain)
+
+
+def per_device(*operands):
+    (patches, patch_counts, dest_rows, qkv_weight, out_weight, attn_gain, merge_gain) = operands[:7]
+    (fc1_weight, fc1_bias, fc2_weight, fc2_bias, text_embeds, section_hidden, llm_gain) = operands[7:]
+    outer, _ = group_bits()
+    group_count = lax.axis_size("section") * lax.axis_size("dp")
+    merged_rows = patches.shape[0] // 4
+    run_cap = merged_rows // group_count
+    seq_rows = text_embeds.shape[0]
+    held = group_count * merged_rows * patches.shape[1] * patches.dtype.itemsize
+    if outer != [("dp", 2), ("section", 1)] or held > KERNEL_BYTES or run_cap % 16 or merged_rows % 128 or seq_rows % 128:
+        return plain_per_device(*operands)
+    width = patches.shape[1]
+    tile_total = patch_counts.shape[0]
+    block_rows = patches.shape[0] // tile_total
+    local_cols = qkv_weight.shape[2]
+    local_heads = local_cols // HEAD_DIM
+    run_total = group_count
+    incoming = from_behind(section_hidden, "section", 1)
+    runs = dest_rows.reshape(run_total, run_cap)
+    run_target = runs[:, 0] // seq_rows
+    takes = jnp.arange(group_count, dtype=jnp.int32)[:, None] == run_target[None, :]
+    tile_slots = block_rows // 4
+    live = (
+        jnp.arange(tile_slots, dtype=jnp.int32)[None, :] * 4 < patch_counts[:, None]
+    ).reshape(run_total, run_cap)
+    place = jnp.where(live, runs % seq_rows - seq_rows, 0)
+    send_place = jnp.sum(jnp.where(takes[:, :, None], place[None], 0), axis=1) + seq_rows
+    my_group = lax.axis_index("section") * lax.axis_size("dp") + lax.axis_index("dp")
+    at_lane = jnp.arange(merged_rows, dtype=jnp.int32)
+    places = jnp.where(
+        (at_lane // run_cap == my_group)[None, :], jnp.tile(send_place, (1, group_count)), 0
+    )[:, None, :]
+
+    def square_sums(value):
+        value = value.astype(jnp.float32)
+        return jnp.sum(value * value, axis=1).reshape(-1, 128)
+
+    sums = jnp.concatenate([square_sums(text_embeds), square_sums(section_hidden)], axis=0)
+
+    normed_in = layer_norm(patches, attn_gain).astype(jnp.bfloat16)
+    projections = jnp.dot(
+        normed_in, qkv_weight.reshape(width, 3 * local_cols), preferred_element_type=jnp.float32
+    ).astype(jnp.bfloat16)
+    projections = projections.reshape(tile_total, block_rows, 3, local_heads, HEAD_DIM)
+    query_part = projections[:, :, 0]
+    key_part = projections[:, :, 1]
+    value_part = projections[:, :, 2]
+    scores = jnp.einsum(
+        "tqhd,tkhd->thqk", query_part, key_part, preferred_element_type=jnp.float32
+    ) * HEAD_DIM ** (-0.5)
+    key_live = (
+        jnp.arange(block_rows, dtype=jnp.int32)[None, None, None, :]
+        < patch_counts[:, None, None, None]
+    )
+    scores = jnp.where(key_live, scores, -1e30)
+    weights = jax.nn.softmax(scores, axis=-1).astype(jnp.bfloat16)
+    attended = jnp.einsum(
+        "thqk,tkhd->tqhd", weights, value_part, preferred_element_type=jnp.float32
+    ).astype(jnp.bfloat16)
+    attended = attended.reshape(patches.shape[0], local_cols)
+    lane_source = jnp.arange(run_total, dtype=jnp.int32)[None, :] * run_cap
+    run_source = jnp.sum(jnp.where(takes, lane_source, 0), axis=1)
+    row_source = (
+        run_source[:, None] + jnp.arange(run_cap, dtype=jnp.int32)[None, :]
+    ).reshape(-1) * 4
+    slots_at = jnp.arange(patches.shape[0], dtype=jnp.int32)
+    patch_at = jnp.arange(4, dtype=jnp.int32)
+    order = (
+        (row_source[None, :] + patch_at[:, None]).reshape(-1)[:, None] == slots_at[None, :]
+    ).astype(jnp.bfloat16)
+    own_order = (
+        (row_source + lax.axis_index("mp"))[:, None] == slots_at[None, :]
+    ).astype(jnp.bfloat16)
+    ordered = jnp.dot(order, attended, preferred_element_type=jnp.float32).astype(jnp.bfloat16)
+    own_patch = jnp.dot(own_order, patches, preferred_element_type=jnp.float32)
+    partial_proj = jnp.dot(ordered, out_weight, preferred_element_type=jnp.float32)
+    own_proj = sum_scatter_mp(
+        partial_proj.astype(jnp.bfloat16).reshape(4, merged_rows, width), 0
+    )
+    block_out = (own_patch + own_proj).astype(jnp.bfloat16)
+    merge_part = layer_norm(block_out, merge_gain).astype(jnp.bfloat16)
+    img, spot, base, total = merger(
+        merge_part,
+        places,
+        sums,
+        fc1_weight,
+        fc1_bias.astype(jnp.float32)[None, :],
+        fc2_weight,
+        fc2_bias.astype(jnp.float32)[None, :],
+    )
+    return placing(
+        text_embeds, incoming, img, spot, total, base.reshape(-1, 1), llm_gain[None, :]
+    )
+
+
 def solution(mesh):
     in_specs = (
         P(("section", "dp"), None),

time: 222 us -> 163 us (0.73)
  Pallas kernels: 150 us -> 125 us
  matrix products: 29.1 us -> 13.1 us
  other arithmetic: 18.4 us -> 10.1 us
  starting transfers between devices: 10.6 us -> 6.39 us
  local copies, waits for them, and re-layouts: 11.6 us -> 7.76 us
    pallas_call x6 -> x1, Pallas kernels: 150 us -> 27.8 us  [vmem_call(): pl.pallas_call(kernel, out_shape=out, in_specs=[pl.BlockSpec(memory_space...]
    pallas_call x0 -> x2, Pallas kernels: none -> 96.9 us  [the longest x1 88.5 us: merger(): pl.pallas_call(merger_kernel, out_shape=(jax.ShapeDtypeStruct((target_row...]
    dot_general x3 -> x0, matrix products: 14.5 us -> none  [the longest x1 6.29 us: per_device(): jnp.dot(hidden, fc2_weight, preferred_element_type=jnp.float32)]
    convert_element_type x5 -> x0, other arithmetic: 6.3 us -> none  [the longest x1 4.13 us: per_device(): layer_inputs = (entering * lax.rsqrt(row_total / HID + llm_eps)[:, None]...]
    all_to_all x1 -> x0, starting transfers between devices: 5.2 us -> none  [per_device(): lax.all_to_all(send_place, ('section', 'dp'), split_axis=0, concat_axis=0...]
    reduce_sum x1 -> x2, other arithmetic: 0.71 us -> 4.25 us  [square_sums(): return jnp.sum(value * value, axis=1).reshape(-1, 128)]
  transfers between devices with their start and end apart: 2 -> 1, of which waited for: 0 -> 0; matrix products, arithmetic and copies ran while one was open for 20% -> 19% of each run, Pallas kernels for 65% -> 71%
where the time goes in v1:
time: 163 us
  Pallas kernels  125 us (77%)
  matrix products  13.1 us (8%)
  other arithmetic  10.1 us (6%)
  local copies, waits for them, and re-layouts  7.76 us (5%)
  starting transfers between devices  6.39 us (4%)
    pallas_call x1, Pallas kernels, merger(): pl.pallas_call(merger_kernel, out_shape=(jax.ShapeDtypeStruct((target_row...  88.5 us
    pallas_call x1, Pallas kernels, vmem_call(): pl.pallas_call(kernel, out_shape=out, in_specs=[pl.BlockSpec(memory_space...  27.8 us
    pallas_call x1, Pallas kernels, placing(): pl.pallas_call(placing_kernel, grid=(rows // height,), out_shape=(jax.Sha...  8.35 us
    ppermute x1, starting transfers between devices, from_behind(): lax.ppermute(value, axis, [(source, source + steps) for source in range(f...  6.39 us
    reduce_sum x2, other arithmetic, square_sums(): return jnp.sum(value * value, axis=1).reshape(-1, 128)  4.25 us
    dot_general x1, matrix products, per_device(): jnp.dot(normed_in, qkv_weight.reshape(width, 3 * local_cols), preferred_e...  3.87 us
    dot_general x1, matrix products, per_device(): jnp.dot(ordered, out_weight, preferred_element_type=jnp.float32)  3.51 us
    sub x1, matrix products, per_device(): weights = jax.nn.softmax(scores, axis=-1).astype(jnp.bfloat16)  3.32 us
  transfers between devices with their start and end apart: 1, of which 0 were waited for; matrix products, arithmetic and copies ran while one was open for 19% of the time, Pallas kernels for 71%

profile of v1, /device:TPU:0, one launch (start us, length us, event | category | flops | bytes accessed | tf_op | source)
XLA Modules:
  0.0 162.8 jit_solution(15016550740194858389)
XLA Ops:
  0.6 0.0 copy-start
  0.6 0.0 copy-start.10
  0.7 6.4 %collective-permute-start = (bf16[512,2048]{1,0:T(8,128)(2,1)}, bf16[512,2048]{1,0:T(8,128)(2,1)}, u32[]{:S(2)}, u32[]{:S(2)}) collective-permute-start(bf16[512,2048]{1,0:T(8,128)(2,1)} %param.26), channel_id=1, source_target_pairs={{0,16},{1,17},{2,18},{3,19},{4,20},{5,21},{6,22},{7,23},{8,24},{9,... | collective-permute-start | bytes 6291464 | tf_op jit(solution)/shard_map/ppermute | solution.py:22
  7.0 2.1 %multiply_reduce_fusion = f32[512]{0:T(512)S(1)} fusion(bf16[512,2048]{1,0:T(8,128)(2,1)} %param.26), kind=kLoop, calls=%fused_computation.1 | loop fusion | flops 3145216 | bytes 2099200 | tf_op jit(solution)/shard_map/reduce_sum | solution.py:1088
  9.1 0.0 copy-done.10
  9.2 0.1 iota_compare_fusion.6
  9.2 0.1 lt.53
  9.3 0.1 lt.54
  9.4 0.0 copy-start.1
  9.4 0.0 copy-start.8
  9.4 0.0 copy-start.9
  9.4 0.0 copy-start.4
  9.4 0.0 copy-start.5
  9.4 0.0 copy-start.6
  9.4 2.2 %multiply_reduce_fusion.1 = f32[512]{0:T(512)S(1)} fusion(bf16[512,2048]{1,0:T(8,128)(2,1)} %text_ref.1), kind=kLoop, calls=%fused_computation.2 | loop fusion | flops 3145216 | bytes 2099200 | tf_op jit(solution)/shard_map/reduce_sum | solution.py:1088
  11.6 0.0 copy-done.1
  11.6 0.2 convert_reduce_fusion
  11.9 0.5 fusion.3
  12.3 0.0 copy-done.8
  12.4 0.6 reshape.285.b1_ref
  13.0 0.0 copy-done.9
  13.0 0.1 reshape.276
  13.0 0.1 slice_reduce_fusion
  13.2 0.1 select_reduce_fusion.1
  13.3 0.1 fusion.23
  13.4 0.1 select_reduce_fusion
  13.5 0.1 add_multiply_fusion
  13.5 0.1 mul.94
  13.6 0.0 copy-done.4
  13.7 0.0 copy-done.5
  13.7 0.0 copy-done.6
  13.7 0.6 broadcast_in_dim.112
  14.3 0.1 tile.10
  14.4 0.0 copy-done
  14.4 3.9 %convolution_convert_fusion.1 = bf16[512,960]{0,1:T(8,128)(2,1)} fusion(bf16[1280,960]{0,1:T(8,128)(2,1)S(1)} %bitcast.48, bf16[512,1280]{1,0:T(8,128)(2,1)} %param.14, f32[1280]{0:T(1024)S(1)} %convert_element_type.53, f32[512]{0:T(512)S(1)} %add_rsqrt_fusion, f32[512]{0:T(512)S(1)} %broadcast_multiply_fusion), kind=kOutput, calls=%fused_computation.19 | convolution fusion | flops 1262059520 | bytes 4760576 | tf_op jit(solution)/shard_map/dot_general | solution.py:1093
  18.3 2.5 %reshape.278 = bf16[2,256,3,4,80]{1,0,4,3,2:T(2,128)(2,1)S(1)} reshape(bf16[512,960]{0,1:T(8,128)(2,1)} %convolution_convert_fusion.1) | data formatting | bytes 1966080 | tf_op jit(solution)/shard_map/reshape | solution.py:1096
  20.8 1.6 fusion.27
  22.3 0.0 copy-start.3
  22.3 3.3 %fusion.28 = (f32[2,4,256]{2,1,0:T(4,128)S(1)}, f32[2,4,256,256]{2,3,1,0:T(8,128)}) fusion(pred[2,256]{1,0:T(4,128)(4,1)S(1)} %iota_compare_fusion.6, bf16[2,256,1,4,80]{1,0,4,3,2:T(2,128)(2,1)} %get-tuple-element.12, bf16[2,256,1,4,80]{1,0,4,3,2:T(2,128)(2,1)} %get-tuple-element.11), kind=kOutput, calls=%fused_computation.74 | convolution fusion | flops 85983488 | bytes 2761216 | tf_op jit(solution)/shard_map/sub | solution.py:1108
  25.7 0.0 copy-done.3
  25.7 1.9 %fusion.13 = bf16[2,256,4,80]{1,3,2,0:T(8,128)(2,1)S(1)} fusion(f32[2,4,256,256]{2,3,1,0:T(8,128)} %get-tuple-element.14, f32[2,4,256]{2,1,0:T(4,128)S(1)} %get-tuple-element.13, bf16[2,256,1,4,80]{1,0,4,3,2:T(2,128)(2,1)S(1)} %copy-done.3), kind=kOutput, calls=%fused_computation.25 | convolution fusion | flops 85098496 | bytes 2760704 | tf_op jit(solution)/shard_map/thqk,tkhd->tqhd/dot_general | solution.py:1109
  27.6 0.3 copy.30
  27.9 3.5 %convolution_convert_fusion = bf16[512,1280]{1,0:T(8,128)(2,1)} fusion(bf16[320,1280]{1,0:T(8,128)(2,1)} %param.18, bf16[512,320]{0,1:T(8,128)(2,1)S(1)} %bitcast.51, s32[512]{0:T(512)S(1)} %add_bitcast_fusion), kind=kOutput, calls=%fused_computation.7 | convolution fusion | flops 588283904 | bytes 2459648 | tf_op jit(solution)/shard_map/dot_general | solution.py:1128
  31.5 27.8 %shard_map.149 = bf16[4,128,1280]{2,1,0:T(8,128)(2,1)} custom-call(bf16[4,128,1280]{2,1,0:T(8,128)(2,1)} %bitcast.57), custom_call_target="tpu_custom_call" | custom-call | flops 26214400000 | bytes 2621440 | tf_op jit(solution)/shard_map/pallas_call | solution.py:37
  59.3 0.0 copy-start.2
  59.3 1.7 %convert_reduce_fusion.1 = f32[128,1280]{1,0:T(8,128)S(1)} fusion(bf16[4,128,1280]{2,1,0:T(8,128)(2,1)} %shard_map.149), kind=kLoop, calls=%fused_computation.11 | loop fusion | flops 1146880 | bytes 1966080 | tf_op jit(solution)/shard_map/reduce_sum | solution.py:176
  61.0 0.0 copy-done.2
  61.0 0.5 fusion.29
  61.5 0.2 multiply_reduce_fusion.2
  61.7 0.6 pad_maximum_fusion.sums_ref
  62.3 0.6 broadcast_select_fusion.place_ref
  62.9 0.9 multiply_convert_fusion
  63.8 0.0 copy-start.7
  63.8 88.5 %shard_map.150 = (bf16[128,2048]{1,0:T(8,128)(2,1)}, s32[1,128]{1,0:T(1,128)}, f32[4,128]{1,0:T(4,128)}, f32[1,128]{1,0:T(1,128)}) custom-call(bf16[4,32,1280]{2,1,0:T(8,128)(2,1)} %bitcast.50, s32[8,1,128]{2,1,0:T(1,128)} %broadcast_select_fusion.place_ref, f32[8,128]{1,0:T(8,128)} %pad_maximum_fusion.sums_ref, bf16[1280,640]{1,0:T(8,128)(2,1)} %w1_ref.1, ...), custom_call_target="tpu_custom_call" | custom-call | flops 99999997952 | bytes 10000000 | tf_op jit(solution)/shard_map/pallas_call | solution.py:939
  152.3 0.0 copy-done.7
  152.3 0.6 broadcast_in_dim.110.gain_ref
  152.9 1.5 copy.31.base_ref
  154.5 0.0 collective-permute-done.incoming_ref
  154.5 8.4 %shard_map.151 = (bf16[512,2048]{1,0:T(8,128)(2,1)}, bf16[512,2048]{1,0:T(8,128)(2,1)}) custom-call(bf16[512,2048]{1,0:T(8,128)(2,1)} %text_ref.1, bf16[512,2048]{1,0:T(8,128)(2,1)} %collective-permute-done.incoming_ref, bf16[128,2048]{1,0:T(8,128)(2,1)} %get-tuple-element.6.img_ref, s32[1,128]{1,0:T(1,128)} %get-tuple-element.7.spot_ref, ...), custom_call_target="tpu_custom_call" | custom-call | flops 1000000000 | bytes 10000000 | tf_op jit(solution)/shard_map/pallas_call | solution.py:1035
  (16 shorter events, 0.1 us)
Async XLA Ops:
  0.6 13.8 %copy-start = (bf16[1280,3,320]{0,2,1:T(8,128)(2,1)S(1)}, bf16[1280,3,320]{0,2,1:T(8,128)(2,1)}, u32[]{:S(2)}) copy-start(bf16[1280,3,320]{0,2,1:T(8,128)(2,1)} %param.17) | copy-start | bytes 7372804
  0.6 8.5 %copy-start.10 = (s32[2]{0:T(128)S(1)}, s32[2]{0:T(128)}, u32[]{:S(2)}) copy-start(s32[2]{0:T(128)} %param.15) | copy-start | bytes 28
  0.7 153.8 %collective-permute-start = (bf16[512,2048]{1,0:T(8,128)(2,1)}, bf16[512,2048]{1,0:T(8,128)(2,1)}, u32[]{:S(2)}, u32[]{:S(2)}) collective-permute-start(bf16[512,2048]{1,0:T(8,128)(2,1)} %param.26), channel_id=1, source_target_pairs={{0,16},{1,17},{2,18},{3,19},{4,20},{5,21},{6,22},{7,23},{8,24},{9,... | collective-permute-start | bytes 6291464 | tf_op jit(solution)/shard_map/ppermute | solution.py:22
  9.4 2.2 %copy-start.1 = (bf16[512,1280]{1,0:T(8,128)(2,1)S(1)}, bf16[512,1280]{1,0:T(8,128)(2,1)}, u32[]{:S(2)}) copy-start(bf16[512,1280]{1,0:T(8,128)(2,1)} %param.14) | copy-start | bytes 3932164
  9.4 3.0 %copy-start.8 = (bf16[640]{0:T(1024)(128)(2,1)S(1)}, bf16[640]{0:T(1024)(128)(2,1)}, u32[]{:S(2)}) copy-start(bf16[640]{0:T(1024)(128)(2,1)} %param.22) | copy-start | bytes 3844
  9.4 3.6 %copy-start.9 = (s32[128]{0:T(128)S(1)}, s32[128]{0:T(128)}, u32[]{:S(2)}) copy-start(s32[128]{0:T(128)} %param.16) | copy-start | bytes 1540
  9.4 4.3 %copy-start.4 = (bf16[1280]{0:T(1024)(128)(2,1)S(1)}, bf16[1280]{0:T(1024)(128)(2,1)}, u32[]{:S(2)}) copy-start(bf16[1280]{0:T(1024)(128)(2,1)} %param.19) | copy-start | bytes 7684
  9.4 4.3 %copy-start.5 = (bf16[1280]{0:T(1024)(128)(2,1)S(1)}, bf16[1280]{0:T(1024)(128)(2,1)}, u32[]{:S(2)}) copy-start(bf16[1280]{0:T(1024)(128)(2,1)} %param.20) | copy-start | bytes 7684
  9.4 4.3 %copy-start.6 = (bf16[2048]{0:T(1024)(128)(2,1)S(1)}, bf16[2048]{0:T(1024)(128)(2,1)}, u32[]{:S(2)}) copy-start(bf16[2048]{0:T(1024)(128)(2,1)} %param.24) | copy-start | bytes 12292
  22.3 3.3 %copy-start.3 = (bf16[2,256,1,4,80]{1,0,4,3,2:T(2,128)(2,1)S(1)}, bf16[2,256,1,4,80]{1,0,4,3,2:T(2,128)(2,1)}, u32[]{:S(2)}) copy-start(bf16[2,256,1,4,80]{1,0,4,3,2:T(2,128)(2,1)} %get-tuple-element.10) | copy-start | bytes 983044
  59.3 1.7 %copy-start.2 = (bf16[512,1280]{1,0:T(8,128)(2,1)S(1)}, bf16[512,1280]{1,0:T(8,128)(2,1)}, u32[]{:S(2)}) copy-start(bf16[512,1280]{1,0:T(8,128)(2,1)} %param.14) | copy-start | bytes 3932164
  63.8 88.5 %copy-start.7 = (bf16[2048]{0:T(1024)(128)(2,1)S(1)}, bf16[2048]{0:T(1024)(128)(2,1)}, u32[]{:S(2)}) copy-start(bf16[2048]{0:T(1024)(128)(2,1)} %param.27) | copy-start | bytes 12292

commit v2 on v1

--- a/solution.py
+++ b/solution.py
@@ -484,7 +484,7 @@
     return (sequence_embeds, layer_inputs)
 
 
-LAG = 2
+LAG = 3
 FC2_COLS = 512
 HALF_ROOT = 0.5**0.5
 
@@ -515,17 +515,41 @@
 
 
 def merger_kernel(
-    x_ref,
+    patches_ref,
+    counts_ref,
+    key_ref,
+    qkv_ref,
+    wo_ref,
+    attn_gain_ref,
+    merge_gain_ref,
     place_ref,
     sums_ref,
-    w1_ref,
+    w1_hbm,
     b1_ref,
-    w2_ref,
+    w2_hbm,
     b2_ref,
     img_ref,
     spot_ref,
     base_ref,
     total_ref,
+    query,
+    key,
+    value_part,
+    attended,
+    ordered,
+    arrived,
+    wo_all,
+    x_ref,
+    w1_ref,
+    w2_ref,
+    weight_sem,
+    wo_send,
+    wo_recv,
+    wo_out,
+    wo_plane,
+    wo_pair,
+    a_send,
+    a_recv,
     rows,
     part,
     before,
@@ -620,8 +644,56 @@
             spot, spot, row_send.at[chunk, 3 + quarter], pair_recv.at[chunk, quarter], pair
         )
 
-    for copy in own_sends(0):
-        copy.start()
+    fetches = [
+        pltpu.make_async_copy(w1_hbm, w1_ref, weight_sem.at[0]),
+        pltpu.make_async_copy(w2_hbm, w2_ref, weight_sem.at[1]),
+    ]
+    for fetch in fetches:
+        fetch.start()
+
+    def wo_slice(ref, holder):
+        high = wo_ref.shape[0] // lax.axis_size("dp")
+        broad = wo_ref.shape[1] // sections
+        top = pl.multiple_of(lax.rem(holder, lax.axis_size("dp")) * high, high)
+        left = pl.multiple_of(holder // lax.axis_size("dp") * broad, broad)
+        return ref.at[pl.ds(top, high), pl.ds(left, broad)]
+
+    def wo_line(step):
+        return remote(
+            wo_slice(wo_ref, group),
+            wo_slice(wo_all.at[me], group),
+            wo_send.at[step - 1],
+            wo_recv.at[step - 1],
+            {"mp": lax.rem(me + step, line)},
+        )
+
+    def wo_hop(step, quarter, at, sem, device):
+        block = wo_slice(wo_all.at[lax.rem(me - step + line, line)], group_of(quarter, core))
+        return remote(block, block, wo_out.at[step - 1, at], sem, device)
+
+    def wo_starts(step):
+        return (
+            wo_hop(step, 0, 0, wo_plane.at[step - 1, 1], over_y),
+            wo_hop(step, 0, 1, wo_plane.at[step - 1, 2], over_x),
+            wo_hop(step, 0, 2, wo_pair.at[step - 1, 0], pair),
+        )
+
+    def wo_forward_x(step):
+        return wo_hop(step, 1, 3, wo_plane.at[step - 1, 3], over_x)
+
+    def wo_forward_pair(step, quarter):
+        return wo_hop(step, quarter, 3 + quarter, wo_pair.at[step - 1, quarter], pair)
+
+    def wo_landed(step, quarter):
+        return wo_hop(step, quarter, 0, wo_plane.at[step - 1, quarter], over_x)
+
+    def wo_paired(step, quarter):
+        block = wo_slice(wo_all.at[lax.rem(me - step + line, line)], group_of(quarter, 1 - core))
+        return remote(block, block, wo_out.at[step - 1, 0], wo_pair.at[step - 1, quarter], pair)
+
+    steps = range(1, line)
+    for step in steps:
+        wo_line(step).start()
 
     place_copies = []
     for step in range(1, groups):
@@ -639,7 +711,97 @@
         sum_copies.append(copy)
     spots[0] = place_ref[group]
     sums[0] = sums_ref[...]
+
+    tall = min(patches_ref.shape[0], 128)
+
+    @pl.loop(0, patches_ref.shape[0] // tall)
+    def _(at):
+        cut = pl.ds(at * tall, tall)
+        normed = layer_norm(patches_ref[cut], attn_gain_ref[...]).astype(jnp.bfloat16)
+        for which, ref in enumerate((query, key, value_part)):
+            ref[cut] = lax.dot_general(
+                normed, qkv_ref[which], (((1,), (1,)), ((), ())), preferred_element_type=jnp.float32
+            ).astype(ref.dtype)
+
+    for step in steps:
+        wo_line(step).wait_recv()
+        for copy in wo_starts(step):
+            copy.start()
+    wo_all[me] = wo_ref[...]
+
+    tiles = counts_ref.shape[0]
+    block = query.shape[0] // tiles
+    lane = lax.broadcasted_iota(jnp.int32, (1, query.shape[1]), 1)
+    at_key = lax.broadcasted_iota(jnp.int32, (block, block), 1)
+
+    def attend(tile):
+        cut = pl.ds(tile * block, block)
+        tile_query, tile_key, tile_value = query[cut], key[cut], value_part[cut]
+        live = at_key < counts_ref[tile]
+        result = jnp.zeros((block, query.shape[1]), jnp.float32)
+        for head in range(query.shape[1] // HEAD_DIM):
+            own = jnp.logical_and(lane >= head * HEAD_DIM, lane < (head + 1) * HEAD_DIM)
+            own = own.astype(jnp.float32).astype(jnp.bfloat16)
+            scores = lax.dot_general(
+                tile_query * own, tile_key, (((1,), (1,)), ((), ())), preferred_element_type=jnp.float32
+            )
+            scores = jnp.where(live, scores * HEAD_DIM**-0.5, -1e30)
+            power = jnp.exp(scores - jnp.max(scores, axis=1, keepdims=True))
+            weights = (power / jnp.sum(power, axis=1, keepdims=True)).astype(jnp.bfloat16)
+            result = result + jnp.dot(weights, tile_value * own, preferred_element_type=jnp.float32)
+        attended[cut] = result.astype(attended.dtype)
+
+    for tile in range(tiles):
+        attend(tile)
+        for step in steps:
+            if tile == 0:
+                wo_landed(step, 1).wait_recv()
+                wo_forward_x(step).start()
+                wo_forward_pair(step, 1).start()
+            elif tile == 1:
+                wo_landed(step, 2).wait_recv()
+                wo_forward_pair(step, 2).start()
+
+    place_of = lax.broadcasted_iota(jnp.int32, (attended.shape[0], attended.shape[0]), 0)
+    order = (key_ref[...] == place_of).astype(jnp.float32).astype(jnp.bfloat16)
+    ordered[...] = (
+        jnp.dot(order, attended[...], preferred_element_type=jnp.float32)
+        .astype(ordered.dtype)
+        .reshape(ordered.shape)
+    )
+
+    def exchange(step):
+        peer = lax.rem(me + step, line)
+        return remote(ordered.at[peer], arrived.at[me], a_send.at[step - 1], a_recv.at[step - 1], {"mp": peer})
+
+    for step in steps:
+        exchange(step).start()
+    arrived[me] = ordered[me]
+    slots = ordered.shape[1]
+    own_place = me * slots + lax.broadcasted_iota(jnp.int32, (slots, attended.shape[0]), 0)
+    own_order = (key_ref[...] == own_place).astype(jnp.float32).astype(jnp.bfloat16)
+    block_out = jnp.dot(own_order, patches_ref[...], preferred_element_type=jnp.float32)
+    for step in steps:
+        wo_landed(step, 3).wait_recv()
+        wo_forward_pair(step, 3).start()
+    for step in steps:
+        for quarter in range(quarters):
+            wo_paired(step, quarter).wait_recv()
+    for step in steps:
+        exchange(step).wait_recv()
+    for source in range(line):
+        block_out = block_out + jnp.dot(
+            arrived[source], wo_all[source], preferred_element_type=jnp.float32
+        )
+    block_out = block_out.astype(jnp.bfloat16)
+    x_ref[...] = (
+        layer_norm(block_out, merge_gain_ref[...]).astype(x_ref.dtype).reshape(x_ref.shape)
+    )
+    for copy in own_sends(0):
+        copy.start()
     rows[group] = x_ref[...]
+    for fetch in fetches:
+        fetch.wait()
 
     def send_right(piece):
         return remote(
@@ -878,6 +1040,14 @@
         copy.start()
         total_copies.append(copy)
 
+    for step in steps:
+        wo_line(step).wait_send()
+        for copy in wo_starts(step) + (wo_forward_x(step),):
+            copy.wait_send()
+        for quarter in range(1, quarters):
+            wo_forward_pair(step, quarter).wait_send()
+        exchange(step).wait_send()
+
     for chunk in range(chips):
         for copy in own_sends(chunk):
             copy.wait_send()
@@ -920,13 +1090,15 @@
     total_ref[...] = row_total
 
 
-def merger(rows, places, sums, w1, b1, w2, b2):
+def merger(patches, counts, keys, qkv, wo, attn_gain, merge_gain, places, sums, w1, b1, w2, b2):
     groups = lax.axis_size("section") * lax.axis_size("dp")
     line = lax.axis_size("mp")
     chips = groups // 2
-    chunk_rows = rows.shape[0] // chips
+    patch_rows, width = patches.shape
+    slot_rows = patch_rows // 4
+    chunk_rows = slot_rows // chips
     run = chunk_rows // 2
-    width = rows.shape[1]
+    local_cols = qkv.shape[1]
     units = w1.shape[1]
     features = w2.shape[1]
     pieces = chips * 4
@@ -944,9 +1116,30 @@
             jax.ShapeDtypeStruct((sum_rows, sums.shape[1]), jnp.float32),
             jax.ShapeDtypeStruct((1, target_rows), jnp.float32),
         ),
-        in_specs=[pl.BlockSpec(memory_space=pltpu.VMEM)] * 7,
+        in_specs=[
+            pl.BlockSpec(memory_space={1: pltpu.SMEM, 9: pl.ANY, 11: pl.ANY}.get(at, pltpu.VMEM))
+            for at in range(13)
+        ],
         out_specs=[pl.BlockSpec(memory_space=pltpu.VMEM)] * 4,
         scratch_shapes=[
+            pltpu.VMEM((patch_rows, local_cols), low),
+            pltpu.VMEM((patch_rows, local_cols), low),
+            pltpu.VMEM((patch_rows, local_cols), low),
+            pltpu.VMEM((patch_rows, local_cols), low),
+            pltpu.VMEM((4, slot_rows, local_cols), low),
+            pltpu.VMEM((line, slot_rows, local_cols), low),
+            pltpu.VMEM((line,) + wo.shape, low),
+            pltpu.VMEM((chips, chunk_rows, width), low),
+            pltpu.VMEM(w1.shape, low),
+            pltpu.VMEM(w2.shape, low),
+            dma((2,)),
+            dma((line - 1,)),
+            dma((line - 1,)),
+            dma((line - 1, 7)),
+            dma((line - 1, 4)),
+            dma((line - 1, 4)),
+            dma((line - 1,)),
+            dma((line - 1,)),
             pltpu.VMEM((groups, chips, chunk_rows, width), low),
             pltpu.VMEM((pieces, piece_rows, units), jnp.float32),
             pltpu.VMEM((pieces, piece_rows, units), low),
@@ -995,7 +1188,7 @@
         compiler_params=pltpu.CompilerParams(
             collective_id=6, has_side_effects=True, vmem_limit_bytes=VMEM_LIMIT
         ),
-    )(rows.reshape(chips, chunk_rows, width), places, sums, w1, b1, w2, b2)
+    )(patches, counts, keys, qkv, wo, attn_gain, merge_gain, places, sums, w1, b1, w2, b2)
 
 
 def placing_kernel(text_ref, incoming_ref, img_ref, spot_ref, total_ref, base_ref, gain_ref, seq_ref, layer_ref):
@@ -1059,13 +1252,10 @@
     run_cap = merged_rows // group_count
     seq_rows = text_embeds.shape[0]
     held = group_count * merged_rows * patches.shape[1] * patches.dtype.itemsize
-    if outer != [("dp", 2), ("section", 1)] or held > KERNEL_BYTES or run_cap % 16 or merged_rows % 128 or seq_rows % 128:
+    if lax.axis_size("mp") != 4 or outer != [("dp", 2), ("section", 1)] or held > KERNEL_BYTES or run_cap % 16 or merged_rows % 128 or seq_rows % 128:
         return plain_per_device(*operands)
-    width = patches.shape[1]
     tile_total = patch_counts.shape[0]
     block_rows = patches.shape[0] // tile_total
-    local_cols = qkv_weight.shape[2]
-    local_heads = local_cols // HEAD_DIM
     run_total = group_count
     incoming = from_behind(section_hidden, "section", 1)
     runs = dest_rows.reshape(run_total, run_cap)
@@ -1089,50 +1279,18 @@
 
     sums = jnp.concatenate([square_sums(text_embeds), square_sums(section_hidden)], axis=0)
 
-    normed_in = layer_norm(patches, attn_gain).astype(jnp.bfloat16)
-    projections = jnp.dot(
-        normed_in, qkv_weight.reshape(width, 3 * local_cols), preferred_element_type=jnp.float32
-    ).astype(jnp.bfloat16)
-    projections = projections.reshape(tile_total, block_rows, 3, local_heads, HEAD_DIM)
-    query_part = projections[:, :, 0]
-    key_part = projections[:, :, 1]
-    value_part = projections[:, :, 2]
-    scores = jnp.einsum(
-        "tqhd,tkhd->thqk", query_part, key_part, preferred_element_type=jnp.float32
-    ) * HEAD_DIM ** (-0.5)
-    key_live = (
-        jnp.arange(block_rows, dtype=jnp.int32)[None, None, None, :]
-        < patch_counts[:, None, None, None]
-    )
-    scores = jnp.where(key_live, scores, -1e30)
-    weights = jax.nn.softmax(scores, axis=-1).astype(jnp.bfloat16)
-    attended = jnp.einsum(
-        "thqk,tkhd->tqhd", weights, value_part, preferred_element_type=jnp.float32
-    ).astype(jnp.bfloat16)
-    attended = attended.reshape(patches.shape[0], local_cols)
-    lane_source = jnp.arange(run_total, dtype=jnp.int32)[None, :] * run_cap
-    run_source = jnp.sum(jnp.where(takes, lane_source, 0), axis=1)
-    row_source = (
-        run_source[:, None] + jnp.arange(run_cap, dtype=jnp.int32)[None, :]
-    ).reshape(-1) * 4
-    slots_at = jnp.arange(patches.shape[0], dtype=jnp.int32)
-    patch_at = jnp.arange(4, dtype=jnp.int32)
-    order = (
-        (row_source[None, :] + patch_at[:, None]).reshape(-1)[:, None] == slots_at[None, :]
-    ).astype(jnp.bfloat16)
-    own_order = (
-        (row_source + lax.axis_index("mp"))[:, None] == slots_at[None, :]
-    ).astype(jnp.bfloat16)
-    ordered = jnp.dot(order, attended, preferred_element_type=jnp.float32).astype(jnp.bfloat16)
-    own_patch = jnp.dot(own_order, patches, preferred_element_type=jnp.float32)
-    partial_proj = jnp.dot(ordered, out_weight, preferred_element_type=jnp.float32)
-    own_proj = sum_scatter_mp(
-        partial_proj.astype(jnp.bfloat16).reshape(4, merged_rows, width), 0
-    )
-    block_out = (own_patch + own_proj).astype(jnp.bfloat16)
-    merge_part = layer_norm(block_out, merge_gain).astype(jnp.bfloat16)
+    slot_key = (
+        run_target[:, None] * run_cap + jnp.arange(run_cap, dtype=jnp.int32)[None, :]
+    ).reshape(-1)
+    keys = (slot_key[:, None] + jnp.arange(4, dtype=jnp.int32)[None, :] * merged_rows).reshape(1, -1)
     img, spot, base, total = merger(
-        merge_part,
+        patches,
+        patch_counts,
+        keys,
+        qkv_weight.transpose(1, 2, 0),
+        out_weight,
+        attn_gain[None, :],
+        merge_gain[None, :],
         places,
         sums,
         fc1_weight,

time: 163 us -> 153 us (0.939)
  matrix products: 13.1 us -> 0 us
  Pallas kernels: 125 us -> 136 us
  other arithmetic: 10.1 us -> 4.89 us
  local copies, waits for them, and re-layouts: 7.76 us -> 5.05 us
    pallas_call x1, Pallas kernels: 88.5 us -> 127 us  [merger(): pl.pallas_call(merger_kernel, out_shape=(jax.ShapeDtypeStruct((target_row...]
    pallas_call x1 -> x0, Pallas kernels: 27.8 us -> none  [vmem_call(): pl.pallas_call(kernel, out_shape=out, in_specs=[pl.BlockSpec(memory_space...]
    dot_general x4 -> x0, matrix products: 9.73 us -> none  [the longest x1 3.87 us: per_device(): jnp.dot(normed_in, qkv_weight.reshape(width, 3 * local_cols), preferred_e...]
    sub x1 -> x0, matrix products: 3.32 us -> none  [per_device(): weights = jax.nn.softmax(scores, axis=-1).astype(jnp.bfloat16)]
    reduce_sum x5 -> x0, other arithmetic: 2.75 us -> none  [the longest x1 1.68 us: sum_scatter_mp(): return jnp.sum(exchange_mp(blocks, True, ident).astype(jnp.float32), axis=0)]
    reshape x1 -> x0, local copies, waits for them, and re-layouts: 2.49 us -> none  [per_device(): projections.reshape(tile_total, block_rows, 3, local_heads, HEAD_DIM)]
    slice x2 -> x0, local copies, waits for them, and re-layouts: 1.69 us -> none  [the longest x1 1.57 us: per_device(): value_part = projections[:, :, 2]]
    reduce_sum x2, other arithmetic: 4.25 us -> 2.6 us  [square_sums(): return jnp.sum(value * value, axis=1).reshape(-1, 128)]
  transfers between devices with their start and end apart: 1 -> 1, of which waited for: 0 -> 0; matrix products, arithmetic and copies ran while one was open for 19% -> 6% of each run, Pallas kernels for 71% -> 83%
where the time goes in v2:
time: 153 us
  Pallas kernels  136 us (89%)
  starting transfers between devices  6.39 us (4%)
  local copies, waits for them, and re-layouts  5.05 us (3%)
  other arithmetic  4.89 us (3%)
    pallas_call x1, Pallas kernels, merger(): pl.pallas_call(merger_kernel, out_shape=(jax.ShapeDtypeStruct((target_row...  127 us
    pallas_call x1, Pallas kernels, placing(): pl.pallas_call(placing_kernel, grid=(rows // height,), out_shape=(jax.Sha...  8.35 us
    ppermute x1, starting transfers between devices, from_behind(): lax.ppermute(value, axis, [(source, source + steps) for source in range(f...  6.39 us
  transfers between devices with their start and end apart: 1, of which 0 were waited for; matrix products, arithmetic and copies ran while one was open for 6% of the time, Pallas kernels for 83%

profile of v2, /device:TPU:0, one launch (start us, length us, event | category | flops | bytes accessed | tf_op | source)
XLA Modules:
  0.0 152.7 jit_solution(4940621528609446278)
XLA Ops:
  0.6 0.0 copy-start.7
  0.6 0.0 copy-start
  0.7 6.4 %collective-permute-start = (bf16[512,2048]{1,0:T(8,128)(2,1)}, bf16[512,2048]{1,0:T(8,128)(2,1)}, u32[]{:S(2)}, u32[]{:S(2)}) collective-permute-start(bf16[512,2048]{1,0:T(8,128)(2,1)} %param.26), channel_id=1, source_target_pairs={{0,16},{1,17},{2,18},{3,19},{4,20},{5,21},{6,22},{7,23},{8,24},{9,... | collective-permute-start | bytes 6291464 | tf_op jit(solution)/shard_map/ppermute | solution.py:22
  7.1 0.0 copy-start.5
  7.1 0.0 copy-start.6
  7.1 0.0 copy-start.3
  7.1 0.0 copy-start.4
  7.1 0.0 copy-start.1
  7.1 2.1 %multiply_reduce_fusion = f32[512]{0:T(512)S(1)} fusion(bf16[512,2048]{1,0:T(8,128)(2,1)} %param.26), kind=kLoop, calls=%fused_computation | loop fusion | flops 3145216 | bytes 2099200 | tf_op jit(solution)/shard_map/reduce_sum | solution.py:1278
  9.2 0.0 copy-done.7
  9.2 0.1 lt.32
  9.3 0.1 lt.33
  9.4 0.0 copy-done
  9.4 0.5 multiply_reduce_fusion.1
  9.9 0.0 copy-done.5
  9.9 0.6 reshape.212.b1_ref
  10.5 0.0 copy-done.6
  10.5 0.1 reshape.208
  10.5 0.2 slice_reduce_fusion
  10.7 0.1 fusion.5
  10.8 0.1 select_reduce_fusion
  10.9 0.1 iota_add_fusion
  11.0 0.1 add.86
  11.1 0.0 copy-done.3
  11.1 0.6 broadcast_in_dim.64.attn_gain_ref
  11.7 0.0 copy-done.4
  11.7 0.6 broadcast_in_dim.65.merge_gain_ref
  12.3 0.0 copy-done.1
  12.3 0.6 broadcast_in_dim.77
  12.9 0.1 tile.10
  13.0 0.1 broadcast_add_fusion
  13.1 0.7 add.90.key_ref
  13.8 0.6 pad_maximum_fusion.sums_ref
  14.3 0.6 broadcast_select_fusion.place_ref
  14.9 0.0 copy-start.2
  14.9 127.3 %shard_map.149 = (bf16[128,2048]{1,0:T(8,128)(2,1)}, s32[1,128]{1,0:T(1,128)}, f32[4,128]{1,0:T(4,128)}, f32[1,128]{1,0:T(1,128)}) custom-call(bf16[512,1280]{1,0:T(8,128)(2,1)} %patches_ref.1, s32[2]{0:T(128)} %counts_ref.1, s32[1,512]{1,0:T(1,128)} %add.90.key_ref, bf16[3,320,1280]{2,1,0:T(8,128)(2,1)} %bitcast.11, bf16[320,1280]{1,0:T(8,128)(2,1)} %wo_ref.1, ...), custom_call_target="tpu_custom_call" | custom-call | flops 99999997952 | bytes 10000000 | tf_op jit(solution)/shard_map/pallas_call | solution.py:1111
  142.2 0.0 copy-done.2
  142.3 0.6 broadcast_in_dim.75.gain_ref
  142.9 1.5 %copy.17.base_ref = f32[512,1]{1,0:T(8,128)} copy(f32[512,1]{0,1:T(1,128)} %bitcast.10) | data formatting | bytes 4096 | tf_op jit(solution)/shard_map/reshape | solution.py:1302
  144.4 0.0 collective-permute-done.incoming_ref
  144.4 8.4 %shard_map.150 = (bf16[512,2048]{1,0:T(8,128)(2,1)}, bf16[512,2048]{1,0:T(8,128)(2,1)}) custom-call(bf16[512,2048]{1,0:T(8,128)(2,1)} %text_ref.1, bf16[512,2048]{1,0:T(8,128)(2,1)} %collective-permute-done.incoming_ref, bf16[128,2048]{1,0:T(8,128)(2,1)} %get-tuple-element.6.img_ref, s32[1,128]{1,0:T(1,128)} %get-tuple-element.7.spot_ref, ...), custom_call_target="tpu_custom_call" | custom-call | flops 1000000000 | bytes 10000000 | tf_op jit(solution)/shard_map/pallas_call | solution.py:1228
  (8 shorter events, 0.0 us)
Async XLA Ops:
  0.6 8.6 %copy-start.7 = (s32[2]{0:T(128)S(1)}, s32[2]{0:T(128)}, u32[]{:S(2)}) copy-start(s32[2]{0:T(128)} %counts_ref.1) | copy-start | bytes 28
  0.6 8.8 %copy-start = (bf16[512,2048]{1,0:T(8,128)(2,1)S(1)}, bf16[512,2048]{1,0:T(8,128)(2,1)}, u32[]{:S(2)}) copy-start(bf16[512,2048]{1,0:T(8,128)(2,1)} %text_ref.1) | copy-start | bytes 6291460
  0.7 143.7 %collective-permute-start = (bf16[512,2048]{1,0:T(8,128)(2,1)}, bf16[512,2048]{1,0:T(8,128)(2,1)}, u32[]{:S(2)}, u32[]{:S(2)}) collective-permute-start(bf16[512,2048]{1,0:T(8,128)(2,1)} %param.26), channel_id=1, source_target_pairs={{0,16},{1,17},{2,18},{3,19},{4,20},{5,21},{6,22},{7,23},{8,24},{9,... | collective-permute-start | bytes 6291464 | tf_op jit(solution)/shard_map/ppermute | solution.py:22
  7.1 2.8 %copy-start.5 = (bf16[640]{0:T(1024)(128)(2,1)S(1)}, bf16[640]{0:T(1024)(128)(2,1)}, u32[]{:S(2)}) copy-start(bf16[640]{0:T(1024)(128)(2,1)} %param.22) | copy-start | bytes 3844
  7.1 3.4 %copy-start.6 = (s32[128]{0:T(128)S(1)}, s32[128]{0:T(128)}, u32[]{:S(2)}) copy-start(s32[128]{0:T(128)} %param.16) | copy-start | bytes 1540
  7.1 4.0 %copy-start.3 = (bf16[1280]{0:T(1024)(128)(2,1)S(1)}, bf16[1280]{0:T(1024)(128)(2,1)}, u32[]{:S(2)}) copy-start(bf16[1280]{0:T(1024)(128)(2,1)} %param.19) | copy-start | bytes 7684
  7.1 4.6 %copy-start.4 = (bf16[1280]{0:T(1024)(128)(2,1)S(1)}, bf16[1280]{0:T(1024)(128)(2,1)}, u32[]{:S(2)}) copy-start(bf16[1280]{0:T(1024)(128)(2,1)} %param.20) | copy-start | bytes 7684
  7.1 5.2 %copy-start.1 = (bf16[2048]{0:T(1024)(128)(2,1)S(1)}, bf16[2048]{0:T(1024)(128)(2,1)}, u32[]{:S(2)}) copy-start(bf16[2048]{0:T(1024)(128)(2,1)} %param.24) | copy-start | bytes 12292
  14.9 127.3 %copy-start.2 = (bf16[2048]{0:T(1024)(128)(2,1)S(1)}, bf16[2048]{0:T(1024)(128)(2,1)}, u32[]{:S(2)}) copy-start(bf16[2048]{0:T(1024)(128)(2,1)} %param.27) | copy-start | bytes 12292

commit v3 on v2

--- a/solution.py
+++ b/solution.py
@@ -517,21 +517,32 @@
 def merger_kernel(
     patches_ref,
     counts_ref,
-    key_ref,
+    dest_ref,
     qkv_ref,
     wo_ref,
     attn_gain_ref,
     merge_gain_ref,
-    place_ref,
-    sums_ref,
     w1_hbm,
     b1_ref,
     w2_hbm,
     b2_ref,
+    text_hbm,
+    carry_hbm,
     img_ref,
     spot_ref,
     base_ref,
     total_ref,
+    incoming_hbm,
+    text_ref,
+    carry_ref,
+    text_squares,
+    carry_squares,
+    carry_sem,
+    carry_send,
+    carry_recv,
+    normed,
+    place_ref,
+    sums_ref,
     query,
     key,
     value_part,
@@ -650,6 +661,30 @@
     ]
     for fetch in fetches:
         fetch.start()
+    leads = section < sections - 1
+    bands = carry_send.shape[0]
+    band_rows = carry_hbm.shape[0] // bands
+    text_fetch = pltpu.make_async_copy(text_hbm, text_ref, carry_sem.at[0])
+    carry_fetch = pltpu.make_async_copy(carry_hbm, carry_ref, carry_sem.at[1])
+
+    @pl.when(leads)
+    def _():
+        text_fetch.start()
+        carry_fetch.start()
+
+    def send_band(at):
+        cut = pl.ds(pl.multiple_of(at * band_rows, band_rows), band_rows)
+        return remote(
+            carry_hbm.at[cut], incoming_hbm.at[cut], carry_send.at[at], carry_recv.at[at], {"section": section + 1}
+        )
+
+    def send_bands(first, last):
+        @pl.when(leads)
+        def _():
+            for at in range(first, last):
+                send_band(at).start()
+
+    early = bands // 8
 
     def wo_slice(ref, holder):
         high = wo_ref.shape[0] // lax.axis_size("dp")
@@ -695,6 +730,36 @@
     for step in steps:
         wo_line(step).start()
 
+    send_bands(0, early)
+    slots = ordered.shape[1]
+    run = slots // groups
+    dest = dest_ref[...].reshape(1, slots)
+    slot = lax.broadcasted_iota(jnp.int32, (1, slots), 1)
+    tiles = counts_ref.shape[0]
+    slice_rows = carry_hbm.shape[0]
+    target = dest // slice_rows
+    slot_place = slot
+    for stride in [1 << bit for bit in range(run.bit_length() - 1, slots.bit_length())][::-1]:
+        slot_place = jnp.where(slot_place >= stride, slot_place - stride, slot_place)
+    slot_target = target * run + slot_place
+    filled = jnp.zeros((1, slots), jnp.int32)
+    for tile in range(tiles):
+        start = tile * (slots // tiles)
+        within = jnp.logical_and(slot >= start, slot - start < slots // tiles)
+        filled = jnp.where(jnp.logical_and(within, (slot - start) * 4 < counts_ref[tile]), 1, filled)
+    spot = jnp.where(filled > 0, dest - target * slice_rows, slice_rows)
+    high = (spot // 16).astype(jnp.float32)
+    low = (spot - spot // 16 * 16).astype(jnp.float32)
+    to_group = lax.broadcasted_iota(jnp.int32, (groups, slots), 0) == target
+    at_source = lax.broadcasted_iota(jnp.int32, (slots, slots), 1)
+    moved = (at_source == group * run + slot_place.reshape(slots, 1)).astype(jnp.float32).astype(jnp.bfloat16)
+
+    def moved_to(value):
+        picked = jnp.where(to_group, value, 0.0).astype(jnp.bfloat16)
+        return jnp.dot(picked, moved, preferred_element_type=jnp.float32)
+
+    place_rows = (moved_to(high) * 16.0 + moved_to(low)).astype(jnp.int32)
+    place_ref[...] = place_rows.reshape(place_ref.shape)
     place_copies = []
     for step in range(1, groups):
         peer = lax.rem(group + step, groups)
@@ -703,33 +768,29 @@
         )
         copy.start()
         place_copies.append(copy)
-    sum_copies = []
-    for step in range(1, line):
-        peer = lax.rem(me + step, line)
-        copy = remote(sums_ref, sums.at[step], sum_send.at[step - 1], sum_recv.at[step - 1], {"mp": peer})
-        copy.start()
-        sum_copies.append(copy)
     spots[0] = place_ref[group]
-    sums[0] = sums_ref[...]
 
     tall = min(patches_ref.shape[0], 128)
 
     @pl.loop(0, patches_ref.shape[0] // tall)
     def _(at):
         cut = pl.ds(at * tall, tall)
-        normed = layer_norm(patches_ref[cut], attn_gain_ref[...]).astype(jnp.bfloat16)
-        for which, ref in enumerate((query, key, value_part)):
-            ref[cut] = lax.dot_general(
-                normed, qkv_ref[which], (((1,), (1,)), ((), ())), preferred_element_type=jnp.float32
-            ).astype(ref.dtype)
+        normed[cut] = layer_norm(
+            patches_ref[cut], attn_gain_ref[...].reshape(1, -1)
+        ).astype(normed.dtype)
+
+    for which, ref in enumerate((query, key, value_part)):
+        ref[...] = lax.dot_general(
+            normed[...], qkv_ref[which], (((1,), (1,)), ((), ())), preferred_element_type=jnp.float32
+        ).astype(ref.dtype)
 
     for step in steps:
         wo_line(step).wait_recv()
         for copy in wo_starts(step):
             copy.start()
+    send_bands(early, 2 * early)
     wo_all[me] = wo_ref[...]
 
-    tiles = counts_ref.shape[0]
     block = query.shape[0] // tiles
     lane = lax.broadcasted_iota(jnp.int32, (1, query.shape[1]), 1)
     at_key = lax.broadcasted_iota(jnp.int32, (block, block), 1)
@@ -761,14 +822,23 @@
             elif tile == 1:
                 wo_landed(step, 2).wait_recv()
                 wo_forward_pair(step, 2).start()
-
-    place_of = lax.broadcasted_iota(jnp.int32, (attended.shape[0], attended.shape[0]), 0)
-    order = (key_ref[...] == place_of).astype(jnp.float32).astype(jnp.bfloat16)
-    ordered[...] = (
-        jnp.dot(order, attended[...], preferred_element_type=jnp.float32)
-        .astype(ordered.dtype)
-        .reshape(ordered.shape)
-    )
+        if tile < 2:
+            send_bands((2 + tile) * early, (3 + tile) * early)
+
+    whole = attended.shape[0]
+    at_row = lax.broadcasted_iota(jnp.int32, (slots, whole), 0)
+    at_patch = lax.broadcasted_iota(jnp.int32, (slots, whole), 1)
+    order = (
+        lax.broadcasted_iota(jnp.int32, (slots, slots), 0) == slot_target
+    ).astype(jnp.float32).astype(jnp.bfloat16)
+
+    def picked(patch, source):
+        pick = (at_patch == at_row * line + patch).astype(jnp.float32).astype(jnp.bfloat16)
+        rows_of = jnp.dot(pick, source, preferred_element_type=jnp.float32).astype(jnp.bfloat16)
+        return jnp.dot(order, rows_of, preferred_element_type=jnp.float32)
+
+    for patch in range(line):
+        ordered[patch] = picked(patch, attended[...]).astype(ordered.dtype)
 
     def exchange(step):
         peer = lax.rem(me + step, line)
@@ -777,10 +847,7 @@
     for step in steps:
         exchange(step).start()
     arrived[me] = ordered[me]
-    slots = ordered.shape[1]
-    own_place = me * slots + lax.broadcasted_iota(jnp.int32, (slots, attended.shape[0]), 0)
-    own_order = (key_ref[...] == own_place).astype(jnp.float32).astype(jnp.bfloat16)
-    block_out = jnp.dot(own_order, patches_ref[...], preferred_element_type=jnp.float32)
+    block_out = picked(me, patches_ref[...])
     for step in steps:
         wo_landed(step, 3).wait_recv()
         wo_forward_pair(step, 3).start()
@@ -795,7 +862,7 @@
         )
     block_out = block_out.astype(jnp.bfloat16)
     x_ref[...] = (
-        layer_norm(block_out, merge_gain_ref[...]).astype(x_ref.dtype).reshape(x_ref.shape)
+        layer_norm(block_out, merge_gain_ref[...].reshape(1, -1)).astype(x_ref.dtype).reshape(x_ref.shape)
     )
     for copy in own_sends(0):
         copy.start()
@@ -850,7 +917,61 @@
                 ).astype(x_out.dtype)
                 send_x(chunk, at).start()
 
+    sum_rows = base_out.shape[0]
+
+    def folded(value):
+        value = value.astype(jnp.float32)
+        square = value * value
+        width = squares.shape[1]
+        total = square[:, :width]
+        for at_col in range(1, square.shape[1] // width):
+            total = total + square[:, at_col * width : (at_col + 1) * width]
+        return total
+
+    def exchange_sums(step):
+        return remote(
+            sums_ref, sums.at[step], sum_send.at[step - 1], sum_recv.at[step - 1], {"mp": lax.rem(me + step, line)}
+        )
+
+    send_base = remote(base_out, base_in, base_send, base_recv, {"section": section + 1})
+    share = text_ref.shape[0] // pieces
+
     def stage(i, carry):
+        @pl.when(jnp.logical_and(leads, i < pieces))
+        def _():
+            @pl.loop(0, (bands - 4 * early) // pieces)
+            def _(at):
+                send_band(4 * early + i * ((bands - 4 * early) // pieces) + at).start()
+
+            @pl.when(i == 0)
+            def _():
+                text_fetch.wait()
+                carry_fetch.wait()
+
+            cut = pl.ds(pl.multiple_of(i * share, share), share)
+            text_squares[cut] = folded(text_ref[cut])
+            carry_squares[cut] = folded(carry_ref[cut])
+
+        @pl.when(jnp.logical_and(leads, i == pieces))
+        def _():
+            for which, ref in enumerate((text_squares, carry_squares)):
+                for at in range(sum_rows):
+                    cut = pl.ds(at * 128, 128)
+                    at_sum = which * sum_rows + at
+                    sums_ref[at_sum : at_sum + 1] = jnp.sum(ref[cut].T, axis=0, keepdims=True)
+            for step in steps:
+                exchange_sums(step).start()
+
+        @pl.when(jnp.logical_and(leads, i == pieces + 4))
+        def _():
+            both = sums_ref[...]
+            for step in steps:
+                exchange_sums(step).wait()
+                both = both + sums[step]
+            base_out[...] = both[sum_rows:]
+            base_ref[...] = both[:sum_rows]
+            send_base.start()
+
         @pl.when(i < pieces)
         def _():
             chunk = i // quarters
@@ -950,7 +1071,7 @@
             def _():
                 part[at_total] = part[at_total] + after[at_total].astype(jnp.float32)
 
-            value = part[at_total] + b1_ref[...]
+            value = part[at_total] + b1_ref[...].reshape(1, -1).astype(jnp.float32)
             value = 0.5 * value * (1.0 + lax.erf(value * HALF_ROOT))
             hidden[chunk, chip_of(quarter)] = value.astype(hidden.dtype).reshape(hidden.shape[2:])
 
@@ -975,20 +1096,6 @@
     lax.fori_loop(0, pieces + 1 + lag_total, stage, 0)
     settle(chips - 1)
 
-    for copy in sum_copies:
-        copy.wait_recv()
-    sum_rows = base_out.shape[0]
-    both = sums[0]
-    for step in range(1, line):
-        both = both + sums[step]
-    base_out[...] = both[sum_rows:]
-    base_ref[...] = both[:sum_rows]
-    send_base = remote(base_out, base_in, base_send, base_recv, {"section": section + 1})
-
-    @pl.when(section < sections - 1)
-    def _():
-        send_base.start()
-
     spot_sum = spots[0]
     for copy in place_copies:
         copy.wait_recv()
@@ -1000,6 +1107,12 @@
     def _():
         send_base.wait_recv()
         base_ref[...] = base_in[...]
+
+        @pl.loop(0, bands)
+        def _(at):
+            remote(
+                carry_hbm.at[pl.ds(0, band_rows)], incoming_hbm.at[pl.ds(0, band_rows)], carry_send.at[at], carry_recv.at[at], over_y
+            ).wait_recv()
 
     own_chunk = section * wide + column
     y_chunk = flip(section, 1) * wide + column
@@ -1020,16 +1133,10 @@
             keep[own_chunk, cut]
             + x_in[own_chunk, cut].astype(jnp.float32)
             + y_in[cut].astype(jnp.float32)
-            + b2_ref[...]
+            + b2_ref[...].reshape(1, -1).astype(jnp.float32)
         ).astype(img_ref.dtype)
         img_ref[cut] = value
-        value = value.astype(jnp.float32)
-        square = value * value
-        width = squares.shape[1]
-        folded = square[:, :width]
-        for at_col in range(1, square.shape[1] // width):
-            folded = folded + square[:, at_col * width : (at_col + 1) * width]
-        squares[cut] = folded
+        squares[cut] = folded(value)
 
     totals[0] = jnp.sum(squares[...].T, axis=0, keepdims=True)
     total_copies = []
@@ -1076,12 +1183,16 @@
         def _(piece):
             send_left(piece).wait_send()
 
-    for copy in place_copies + sum_copies:
+    for copy in place_copies:
         copy.wait_send()
 
-    @pl.when(section < sections - 1)
+    @pl.when(leads)
     def _():
         send_base.wait_send()
+
+        @pl.loop(0, bands)
+        def _(at):
+            send_band(at).wait_send()
 
     row_total = totals[0]
     for step, copy in enumerate(total_copies):
@@ -1090,7 +1201,7 @@
     total_ref[...] = row_total
 
 
-def merger(patches, counts, keys, qkv, wo, attn_gain, merge_gain, places, sums, w1, b1, w2, b2):
+def merger(patches, counts, dest, qkv, wo, attn_gain, merge_gain, w1, b1, w2, b2, text, carry):
     groups = lax.axis_size("section") * lax.axis_size("dp")
     line = lax.axis_size("mp")
     chips = groups // 2
@@ -1107,21 +1218,33 @@
     parts = 4
     low = jnp.bfloat16
     dma = pltpu.SemaphoreType.DMA
-    sum_rows = sums.shape[0] // 2
+    sum_rows = text.shape[0] // 128
+    bands = text.shape[0] // 16
     return pl.pallas_call(
         merger_kernel,
         out_shape=(
             jax.ShapeDtypeStruct((target_rows, features), low),
-            jax.ShapeDtypeStruct(places.shape[1:], jnp.int32),
-            jax.ShapeDtypeStruct((sum_rows, sums.shape[1]), jnp.float32),
+            jax.ShapeDtypeStruct((1, slot_rows), jnp.int32),
+            jax.ShapeDtypeStruct((sum_rows, 128), jnp.float32),
             jax.ShapeDtypeStruct((1, target_rows), jnp.float32),
+            jax.ShapeDtypeStruct(carry.shape, carry.dtype),
         ),
         in_specs=[
-            pl.BlockSpec(memory_space={1: pltpu.SMEM, 9: pl.ANY, 11: pl.ANY}.get(at, pltpu.VMEM))
+            pl.BlockSpec(memory_space={1: pltpu.SMEM, 7: pl.ANY, 9: pl.ANY, 11: pl.ANY, 12: pl.ANY}.get(at, pltpu.VMEM))
             for at in range(13)
         ],
-        out_specs=[pl.BlockSpec(memory_space=pltpu.VMEM)] * 4,
+        out_specs=[pl.BlockSpec(memory_space=pltpu.VMEM)] * 4 + [pl.BlockSpec(memory_space=pl.ANY)],
         scratch_shapes=[
+            pltpu.VMEM(text.shape, low),
+            pltpu.VMEM(text.shape, low),
+            pltpu.VMEM((text.shape[0], 128), jnp.float32),
+            pltpu.VMEM((text.shape[0], 128), jnp.float32),
+            dma((2,)),
+            dma((bands,)),
+            dma((bands,)),
+            pltpu.VMEM(patches.shape, low),
+            pltpu.VMEM((groups, 1, slot_rows), jnp.int32),
+            pltpu.VMEM((2 * sum_rows, 128), jnp.float32),
             pltpu.VMEM((patch_rows, local_cols), low),
             pltpu.VMEM((patch_rows, local_cols), low),
             pltpu.VMEM((patch_rows, local_cols), low),
@@ -1155,10 +1278,10 @@
             pltpu.VMEM((target_rows, features), low),
             pltpu.VMEM((target_rows, features), low),
             pltpu.VMEM((target_rows, 128), jnp.float32),
-            pltpu.VMEM(places.shape, jnp.int32),
-            pltpu.VMEM((line,) + sums.shape, jnp.float32),
-            pltpu.VMEM((sum_rows, sums.shape[1]), jnp.float32),
-            pltpu.VMEM((sum_rows, sums.shape[1]), jnp.float32),
+            pltpu.VMEM((groups, 1, slot_rows), jnp.int32),
+            pltpu.VMEM((line, 2 * sum_rows, 128), jnp.float32),
+            pltpu.VMEM((sum_rows, 128), jnp.float32),
+            pltpu.VMEM((sum_rows, 128), jnp.float32),
             pltpu.VMEM((line, 1, target_rows), jnp.float32),
             dma((chips, 7)),
             dma((chips, 4)),
@@ -1188,58 +1311,96 @@
         compiler_params=pltpu.CompilerParams(
             collective_id=6, has_side_effects=True, vmem_limit_bytes=VMEM_LIMIT
         ),
-    )(patches, counts, keys, qkv, wo, attn_gain, merge_gain, places, sums, w1, b1, w2, b2)
-
-
-def placing_kernel(text_ref, incoming_ref, img_ref, spot_ref, total_ref, base_ref, gain_ref, seq_ref, layer_ref):
-    height = text_ref.shape[0]
-    at_row = pl.program_id(0) * height + lax.broadcasted_iota(jnp.int32, (height, spot_ref.shape[1]), 0)
-    hits = spot_ref[...] == at_row
-    hit = jnp.max(hits.astype(jnp.float32), axis=1, keepdims=True) > 0.0
-    placed = jnp.dot(
-        hits.astype(jnp.bfloat16), img_ref[...], preferred_element_type=jnp.float32
-    ).astype(jnp.bfloat16)
-    sequence = jnp.where(hit, placed, text_ref[...])
-    seq_ref[...] = sequence
-    gain = gain_ref[...].astype(jnp.float32)
-    base = base_ref[...]
-
-    @pl.when(lax.axis_index("section") == 0)
-    def _():
-        total = jnp.sum(jnp.where(hits, total_ref[...], 0.0), axis=1, keepdims=True)
-        total = jnp.where(hit, total, base)
-        scale = lax.rsqrt(total / HID + llm_eps)
-        layer_ref[...] = (sequence.astype(jnp.float32) * scale * gain).astype(layer_ref.dtype)
-
-    @pl.when(lax.axis_index("section") > 0)
-    def _():
-        scale = lax.rsqrt(base / HID + llm_eps)
-        layer_ref[...] = (incoming_ref[...].astype(jnp.float32) * scale * gain).astype(layer_ref.dtype)
+    )(patches, counts, dest, qkv, wo, attn_gain, merge_gain, w1, b1, w2, b2, text, carry)
+
+
+def placing_kernel(
+    text_hbm,
+    incoming_hbm,
+    img_ref,
+    spot_ref,
+    total_ref,
+    base_ref,
+    gain_ref,
+    seq_hbm,
+    layer_hbm,
+    text,
+    incoming,
+    seq,
+    layer,
+    load_sem,
+    store_sem,
+):
+    cuts = base_ref.shape[0]
+    height = text.shape[0] // cuts
+    first = lax.axis_index("section") == 0
+    gain = gain_ref[...].reshape(1, -1).astype(jnp.float32)
+
+    def move(which, at):
+        cut = pl.ds(at * height, height)
+        source, target, sem = (
+            (text_hbm, text, load_sem.at[0, at]),
+            (incoming_hbm, incoming, load_sem.at[1, at]),
+            (seq, seq_hbm, store_sem.at[0, at]),
+            (layer, layer_hbm, store_sem.at[1, at]),
+        )[which]
+        return pltpu.make_async_copy(source.at[cut], target.at[cut], sem)
+
+    for at in range(cuts):
+        move(0, at).start()
+
+        @pl.when(jnp.logical_not(first))
+        def _():
+            move(1, at).start()
+
+    width = base_ref.shape[1]
+    diagonal = lax.broadcasted_iota(jnp.int32, (height, width), 0) == lax.broadcasted_iota(
+        jnp.int32, (height, width), 1
+    )
+    for at in range(cuts):
+        cut = pl.ds(at * height, height)
+        at_row = at * height + lax.broadcasted_iota(jnp.int32, (height, spot_ref.shape[1]), 0)
+        hits = spot_ref[...] == at_row
+        hit = jnp.max(hits.astype(jnp.float32), axis=1, keepdims=True) > 0.0
+        placed = jnp.dot(
+            hits.astype(jnp.float32).astype(jnp.bfloat16), img_ref[...], preferred_element_type=jnp.float32
+        ).astype(jnp.bfloat16)
+        base = jnp.sum(jnp.where(diagonal, base_ref[at : at + 1], 0.0), axis=1, keepdims=True)
+        move(0, at).wait()
+        seq[cut] = jnp.where(hit, placed, text[cut])
+        move(2, at).start()
+
+        @pl.when(first)
+        def _():
+            total = jnp.sum(jnp.where(hits, total_ref[...], 0.0), axis=1, keepdims=True)
+            total = jnp.where(hit, total, base)
+            scale = lax.rsqrt(total / HID + llm_eps)
+            layer[cut] = (seq[cut].astype(jnp.float32) * scale * gain).astype(layer.dtype)
+
+        @pl.when(jnp.logical_not(first))
+        def _():
+            move(1, at).wait()
+            scale = lax.rsqrt(base / HID + llm_eps)
+            layer[cut] = (incoming[cut].astype(jnp.float32) * scale * gain).astype(layer.dtype)
+
+        move(3, at).start()
+
+    for at in range(cuts):
+        move(2, at).wait()
+        move(3, at).wait()
 
 
 def placing(text, incoming, img, spot, total, base, gain):
-    rows, features = text.shape
-    height = rows // 8
-    block = pl.BlockSpec((height, features), lambda i: (i, 0))
-
-    def whole(value):
-        return pl.BlockSpec(value.shape, lambda i: (0, 0))
-
+    cuts = base.shape[0]
     return pl.pallas_call(
         placing_kernel,
-        grid=(rows // height,),
         out_shape=(jax.ShapeDtypeStruct(text.shape, text.dtype),) * 2,
-        in_specs=[
-            block,
-            block,
-            whole(img),
-            whole(spot),
-            whole(total),
-            pl.BlockSpec((height, 1), lambda i: (i, 0)),
-            whole(gain),
-        ],
-        out_specs=(block, block),
+        in_specs=[pl.BlockSpec(memory_space=pl.ANY)] * 2 + [pl.BlockSpec(memory_space=pltpu.VMEM)] * 5,
+        out_specs=[pl.BlockSpec(memory_space=pl.ANY)] * 2,
+        scratch_shapes=[pltpu.VMEM(text.shape, text.dtype)] * 4
+        + [pltpu.SemaphoreType.DMA((2, cuts)), pltpu.SemaphoreType.DMA((2, cuts))],
         cost_estimate=pl.CostEstimate(flops=10**9, bytes_accessed=10**7, transcendentals=0),
+        compiler_params=pltpu.CompilerParams(vmem_limit_bytes=VMEM_LIMIT),
     )(text, incoming, img, spot, total, base, gain)
 
 
@@ -1254,53 +1415,22 @@
     held = group_count * merged_rows * patches.shape[1] * patches.dtype.itemsize
     if lax.axis_size("mp") != 4 or outer != [("dp", 2), ("section", 1)] or held > KERNEL_BYTES or run_cap % 16 or merged_rows % 128 or seq_rows % 128:
         return plain_per_device(*operands)
-    tile_total = patch_counts.shape[0]
-    block_rows = patches.shape[0] // tile_total
-    run_total = group_count
-    incoming = from_behind(section_hidden, "section", 1)
-    runs = dest_rows.reshape(run_total, run_cap)
-    run_target = runs[:, 0] // seq_rows
-    takes = jnp.arange(group_count, dtype=jnp.int32)[:, None] == run_target[None, :]
-    tile_slots = block_rows // 4
-    live = (
-        jnp.arange(tile_slots, dtype=jnp.int32)[None, :] * 4 < patch_counts[:, None]
-    ).reshape(run_total, run_cap)
-    place = jnp.where(live, runs % seq_rows - seq_rows, 0)
-    send_place = jnp.sum(jnp.where(takes[:, :, None], place[None], 0), axis=1) + seq_rows
-    my_group = lax.axis_index("section") * lax.axis_size("dp") + lax.axis_index("dp")
-    at_lane = jnp.arange(merged_rows, dtype=jnp.int32)
-    places = jnp.where(
-        (at_lane // run_cap == my_group)[None, :], jnp.tile(send_place, (1, group_count)), 0
-    )[:, None, :]
-
-    def square_sums(value):
-        value = value.astype(jnp.float32)
-        return jnp.sum(value * value, axis=1).reshape(-1, 128)
-
-    sums = jnp.concatenate([square_sums(text_embeds), square_sums(section_hidden)], axis=0)
-
-    slot_key = (
-        run_target[:, None] * run_cap + jnp.arange(run_cap, dtype=jnp.int32)[None, :]
-    ).reshape(-1)
-    keys = (slot_key[:, None] + jnp.arange(4, dtype=jnp.int32)[None, :] * merged_rows).reshape(1, -1)
-    img, spot, base, total = merger(
+    img, spot, base, total, incoming = merger(
         patches,
         patch_counts,
-        keys,
+        dest_rows,
         qkv_weight.transpose(1, 2, 0),
         out_weight,
-        attn_gain[None, :],
-        merge_gain[None, :],
-        places,
-        sums,
+        attn_gain,
+        merge_gain,
         fc1_weight,
-        fc1_bias.astype(jnp.float32)[None, :],
+        fc1_bias,
         fc2_weight,
-        fc2_bias.astype(jnp.float32)[None, :],
-    )
-    return placing(
-        text_embeds, incoming, img, spot, total, base.reshape(-1, 1), llm_gain[None, :]
-    )
+        fc2_bias,
+        text_embeds,
+        section_hidden,
+    )
+    return placing(text_embeds, incoming, img, spot, total, base, llm_gain)
 
 
 def solution(mesh):

time: 153 us -> 114 us (0.75)
  Pallas kernels: 136 us -> 113 us
  starting transfers between devices: 6.39 us -> 0 us
  local copies, waits for them, and re-layouts: 5.05 us -> 0 us
  other arithmetic: 4.89 us -> 0 us
    pallas_call x1, Pallas kernels: 127 us -> 108 us  [merger(): pl.pallas_call(merger_kernel, out_shape=(jax.ShapeDtypeStruct((target_row...]
    ppermute x1 -> x0, starting transfers between devices: 6.39 us -> none  [from_behind(): lax.ppermute(value, axis, [(source, source + steps) for source in range(f...]
    pallas_call x1, Pallas kernels: 8.35 us -> 5.02 us  [placing(): pl.pallas_call(placing_kernel, out_shape=(jax.ShapeDtypeStruct(text.shape...]
    reduce_sum x3 -> x0, other arithmetic: 2.69 us -> none  [the longest x2 2.6 us: square_sums(): return jnp.sum(value * value, axis=1).reshape(-1, 128)]
    broadcast_in_dim x4 -> x0, local copies, waits for them, and re-layouts: 2.38 us -> none  [the longest x1 0.6 us: per_device(): llm_gain[None, :]]
    reshape x2 -> x0, local copies, waits for them, and re-layouts: 1.61 us -> none  [the longest x1 1.53 us: per_device(): base.reshape(-1, 1)]
  transfers between devices with their start and end apart: 1 -> 0, of which waited for: 0 -> 0; matrix products, arithmetic and copies ran while one was open for 6% -> 0% of each run, Pallas kernels for 83% -> 0%
where the time goes in v3:
time: 114 us
  Pallas kernels  113 us (99%)
    pallas_call x1, Pallas kernels, merger(): pl.pallas_call(merger_kernel, out_shape=(jax.ShapeDtypeStruct((target_row...  108 us
    pallas_call x1, Pallas kernels, placing(): pl.pallas_call(placing_kernel, out_shape=(jax.ShapeDtypeStruct(text.shape...  5.02 us

profile of v3, /device:TPU:0, one launch (start us, length us, event | category | flops | bytes accessed | tf_op | source)
XLA Modules:
  0.0 113.7 jit_solution(465615126759191925)
XLA Ops:
  0.6 108.0 %shard_map.149 = (bf16[128,2048]{1,0:T(8,128)(2,1)}, s32[1,128]{1,0:T(1,128)}, f32[4,128]{1,0:T(4,128)}, f32[1,128]{1,0:T(1,128)}, bf16[512,2048]{1,0:T(8,128)(2,1)}) custom-call(bf16[512,1280]{1,0:T(8,128)(2,1)} %patches_ref.1, s32[2]{0:T(128)} %counts_ref.1, s32[128]{0:T(128)} %dest_ref.1, bf16[3,320,1280]{2,1,0:T(8,128)(2,1)} %bitcast.1, ...), custom_call_target="tpu_custom_call" | custom-call | flops 99999997952 | bytes 10000000 | tf_op jit(solution)/shard_map/pallas_call | solution.py:1223
  108.7 5.0 %shard_map.150 = (bf16[512,2048]{1,0:T(8,128)(2,1)}, bf16[512,2048]{1,0:T(8,128)(2,1)}) custom-call(bf16[512,2048]{1,0:T(8,128)(2,1)} %text_hbm.3, bf16[512,2048]{1,0:T(8,128)(2,1)} %get-tuple-element.7.incoming_hbm, bf16[128,2048]{1,0:T(8,128)(2,1)} %get-tuple-element.8.img_ref, s32[1,128]{1,0:T(1,128)} %get-tuple-element.9.spot_ref, ...), custom_call_target="tpu_custom_call" | custom-call | flops 1000000000 | bytes 10000000 | tf_op jit(solution)/shard_map/pallas_call | solution.py:1395

commit v4 on v3

--- a/solution.py
+++ b/solution.py
@@ -515,11 +515,11 @@
 
 
 def merger_kernel(
-    patches_ref,
+    patches_hbm,
     counts_ref,
     dest_ref,
-    qkv_ref,
-    wo_ref,
+    qkv_hbm,
+    wo_hbm,
     attn_gain_ref,
     merge_gain_ref,
     w1_hbm,
@@ -533,6 +533,9 @@
     base_ref,
     total_ref,
     incoming_hbm,
+    patches_ref,
+    qkv_ref,
+    wo_ref,
     text_ref,
     carry_ref,
     text_squares,
@@ -621,9 +624,27 @@
     pieces = chips * quarters
     take_rows = rows.shape[2] // 2
     lag_right = me * LAG
+    half_rows = part.shape[3]
+    split_from = 2
+    single = 6
+    run = half_rows // 2
     lag_left = (line - 1 - me) * LAG
     lag_total = (line - 1) * LAG
 
+    fetches = [
+        pltpu.make_async_copy(source, target, weight_sem.at[at])
+        for at, (source, target) in enumerate(
+            (
+                (wo_hbm, wo_ref),
+                (patches_hbm, patches_ref),
+                (qkv_hbm, qkv_ref),
+                (w1_hbm, w1_ref),
+                (w2_hbm, w2_ref),
+            )
+        )
+    ]
+    for fetch in fetches:
+        fetch.start()
     for step in range(1, groups):
         tell(group_device(lax.rem(group + step, groups)))
     for step in range(1, line):
@@ -638,12 +659,10 @@
     def group_of(quarter, at_core):
         return chip_of(quarter) * 2 + at_core
 
-    def own_sends(chunk):
-        return (
-            remote(x_ref.at[chunk], rows.at[group, chunk], row_send.at[chunk, 0], row_recv.at[chunk, 1], over_y),
-            remote(x_ref.at[chunk], rows.at[group, chunk], row_send.at[chunk, 1], row_recv.at[chunk, 2], over_x),
-            remote(x_ref.at[chunk], rows.at[group, chunk], row_send.at[chunk, 2], pair_recv.at[chunk, 0], pair),
-        )
+    def own_send(chunk, which):
+        sem = (row_recv.at[chunk, 1], row_recv.at[chunk, 2], pair_recv.at[chunk, 0])[which]
+        device = (over_y, over_x, pair)[which]
+        return remote(x_ref.at[chunk], rows.at[group, chunk], row_send.at[chunk, which], sem, device)
 
     def forward_x(chunk):
         spot = rows.at[group_of(1, core), chunk]
@@ -655,12 +674,6 @@
             spot, spot, row_send.at[chunk, 3 + quarter], pair_recv.at[chunk, quarter], pair
         )
 
-    fetches = [
-        pltpu.make_async_copy(w1_hbm, w1_ref, weight_sem.at[0]),
-        pltpu.make_async_copy(w2_hbm, w2_ref, weight_sem.at[1]),
-    ]
-    for fetch in fetches:
-        fetch.start()
     leads = section < sections - 1
     bands = carry_send.shape[0]
     band_rows = carry_hbm.shape[0] // bands
@@ -684,7 +697,8 @@
             for at in range(first, last):
                 send_band(at).start()
 
-    early = bands // 8
+    early = bands // 10
+    looped = bands - early - bands // 6
 
     def wo_slice(ref, holder):
         high = wo_ref.shape[0] // lax.axis_size("dp")
@@ -727,12 +741,19 @@
         return remote(block, block, wo_out.at[step - 1, 0], wo_pair.at[step - 1, quarter], pair)
 
     steps = range(1, line)
-    for step in steps:
+    low_end, high_end = me == 0, me == line - 1
+    at_end = jnp.logical_or(low_end, high_end)
+    first_sent = jnp.where(high_end, 3, 1)
+    second = jnp.where(at_end, 2, 3)
+    last_sent = jnp.where(low_end, 3, jnp.where(high_end, 1, 2))
+    first_here = jnp.where(low_end, 3, 1)
+    last_here = jnp.where(low_end, 1, jnp.where(high_end, 3, 2))
+    fetches[0].wait()
+    for step in (first_sent, second, last_sent):
         wo_line(step).start()
 
     send_bands(0, early)
     slots = ordered.shape[1]
-    run = slots // groups
     dest = dest_ref[...].reshape(1, slots)
     slot = lax.broadcasted_iota(jnp.int32, (1, slots), 1)
     tiles = counts_ref.shape[0]
@@ -771,6 +792,7 @@
     spots[0] = place_ref[group]
 
     tall = min(patches_ref.shape[0], 128)
+    fetches[1].wait()
 
     @pl.loop(0, patches_ref.shape[0] // tall)
     def _(at):
@@ -779,16 +801,27 @@
             patches_ref[cut], attn_gain_ref[...].reshape(1, -1)
         ).astype(normed.dtype)
 
+    fetches[2].wait()
     for which, ref in enumerate((query, key, value_part)):
         ref[...] = lax.dot_general(
             normed[...], qkv_ref[which], (((1,), (1,)), ((), ())), preferred_element_type=jnp.float32
         ).astype(ref.dtype)
 
-    for step in steps:
+    def begin(step):
         wo_line(step).wait_recv()
         for copy in wo_starts(step):
             copy.start()
-    send_bands(early, 2 * early)
+
+    def pass_y(step):
+        wo_landed(step, 1).wait_recv()
+        wo_forward_x(step).start()
+        wo_forward_pair(step, 1).start()
+
+    def pass_x(step, quarter):
+        wo_landed(step, quarter).wait_recv()
+        wo_forward_pair(step, quarter).start()
+
+    begin(first_here)
     wo_all[me] = wo_ref[...]
 
     block = query.shape[0] // tiles
@@ -814,16 +847,11 @@
 
     for tile in range(tiles):
         attend(tile)
-        for step in steps:
-            if tile == 0:
-                wo_landed(step, 1).wait_recv()
-                wo_forward_x(step).start()
-                wo_forward_pair(step, 1).start()
-            elif tile == 1:
-                wo_landed(step, 2).wait_recv()
-                wo_forward_pair(step, 2).start()
-        if tile < 2:
-            send_bands((2 + tile) * early, (3 + tile) * early)
+        if tile == 0:
+            begin(second)
+    pass_y(first_here)
+    begin(last_here)
+    send_bands(early, bands - looped)
 
     whole = attended.shape[0]
     at_row = lax.broadcasted_iota(jnp.int32, (slots, whole), 0)
@@ -848,9 +876,14 @@
         exchange(step).start()
     arrived[me] = ordered[me]
     block_out = picked(me, patches_ref[...])
-    for step in steps:
-        wo_landed(step, 3).wait_recv()
-        wo_forward_pair(step, 3).start()
+    pass_y(second)
+    pass_x(first_here, 2)
+    pass_y(last_here)
+    pass_x(second, 2)
+    pass_x(first_here, 3)
+    pass_x(last_here, 2)
+    pass_x(second, 3)
+    pass_x(last_here, 3)
     for step in steps:
         for quarter in range(quarters):
             wo_paired(step, quarter).wait_recv()
@@ -864,10 +897,12 @@
     x_ref[...] = (
         layer_norm(block_out, merge_gain_ref[...].reshape(1, -1)).astype(x_ref.dtype).reshape(x_ref.shape)
     )
-    for copy in own_sends(0):
-        copy.start()
+    for chunk in range(chips):
+        own_send(chunk, 0).start()
+    for which in (1, 2):
+        own_send(0, which).start()
     rows[group] = x_ref[...]
-    for fetch in fetches:
+    for fetch in fetches[3:]:
         fetch.wait()
 
     def send_right(piece):
@@ -937,12 +972,15 @@
     share = text_ref.shape[0] // pieces
 
     def stage(i, carry):
+        for extra in range(2):
+            band = bands - looped + (i - quarters) * 2 + extra
+
+            @pl.when(jnp.logical_and(leads, jnp.logical_and(i >= quarters, band < bands)))
+            def _():
+                send_band(band).start()
+
         @pl.when(jnp.logical_and(leads, i < pieces))
         def _():
-            @pl.loop(0, (bands - 4 * early) // pieces)
-            def _(at):
-                send_band(4 * early + i * ((bands - 4 * early) // pieces) + at).start()
-
             @pl.when(i == 0)
             def _():
                 text_fetch.wait()
@@ -972,10 +1010,9 @@
             base_ref[...] = both[:sum_rows]
             send_base.start()
 
-        @pl.when(i < pieces)
-        def _():
-            chunk = i // quarters
-            quarter = lax.rem(i, quarters)
+        def relay(piece):
+            chunk = piece // quarters
+            quarter = lax.rem(piece, quarters)
 
             @pl.when(quarter == 1)
             def _():
@@ -987,8 +1024,8 @@
 
                 @pl.when(chunk + 1 < chips)
                 def _():
-                    for copy in own_sends(chunk + 1):
-                        copy.start()
+                    for which in (1, 2):
+                        own_send(chunk + 1, which).start()
 
             @pl.when(quarter > 1)
             def _():
@@ -997,17 +1034,42 @@
                 ).wait_recv()
                 forward_pair(chunk, quarter).start()
 
-        at_dot = i - 1
-
-        @pl.when(jnp.logical_and(at_dot >= 0, at_dot < pieces))
-        def _():
-            chunk = at_dot // quarters
-            quarter = lax.rem(at_dot, quarters)
+        def multiply(piece):
+            chunk = piece // quarters
+            quarter = lax.rem(piece, quarters)
             spot = rows.at[group_of(quarter, 1 - core), chunk]
             remote(x_ref.at[chunk], spot, row_send.at[chunk, 2], pair_recv.at[chunk, quarter], pair).wait_recv()
             lhs = rows[pl.ds(chip_of(quarter) * 2, 2), chunk]
-            part[at_dot] = jnp.dot(
-                lhs.reshape(part.shape[1], lhs.shape[2]), w1_ref[...], preferred_element_type=jnp.float32
+            result = jnp.dot(
+                lhs.reshape(-1, lhs.shape[2]), w1_ref[...], preferred_element_type=jnp.float32
+            ).reshape(2, 2, run, part.shape[4])
+            for target in range(2):
+                part[chunk, quarter, target] = result[:, target].reshape(part.shape[3:])
+
+        def once_then_twice(turn, work):
+            @pl.when(jnp.logical_and(turn >= 0, turn < single))
+            def _():
+                work(turn)
+
+            @pl.when(jnp.logical_and(turn >= single, turn < (pieces + single) // 2))
+            def _():
+                work(turn * 2 - single)
+                work(turn * 2 - single + 1)
+
+        once_then_twice(i, relay)
+        once_then_twice(i - 1, multiply)
+
+        def halves(piece):
+            chunk = piece // quarters
+            turn = lax.rem(piece, quarters)
+            first_quarter = jnp.where(chunk < split_from, turn, lax.rem(turn, 2) * 2)
+            last_quarter = jnp.where(chunk < split_from, turn, lax.rem(turn, 2) * 2 + 1)
+            first_target = jnp.where(chunk < split_from, 0, turn // 2)
+            last_target = jnp.where(chunk < split_from, 1, turn // 2)
+            low_half, high_half = pl.ds(0, half_rows), pl.ds(half_rows, half_rows)
+            return (
+                (low_half, (chunk, first_quarter, first_target)),
+                (high_half, (chunk, last_quarter, last_target)),
             )
 
         at_right = i - 1 - lag_right
@@ -1016,14 +1078,16 @@
         def _():
             @pl.when(me == 0)
             def _():
-                right_out[at_right] = part[at_right].astype(right_out.dtype)
+                for cut, spot in halves(at_right):
+                    right_out[at_right, cut] = part[spot].astype(right_out.dtype)
 
             @pl.when(me > 0)
             def _():
                 send_right(at_right).wait_recv()
-                right_out[at_right] = (
-                    part[at_right] + before[at_right].astype(jnp.float32)
-                ).astype(right_out.dtype)
+                for cut, spot in halves(at_right):
+                    right_out[at_right, cut] = (
+                        part[spot] + before[at_right, cut].astype(jnp.float32)
+                    ).astype(right_out.dtype)
 
             send_right(at_right).start()
 
@@ -1033,14 +1097,16 @@
         def _():
             @pl.when(me == line - 1)
             def _():
-                left_out[at_left] = part[at_left].astype(left_out.dtype)
+                for cut, spot in halves(at_left):
+                    left_out[at_left, cut] = part[spot].astype(left_out.dtype)
 
             @pl.when(me < line - 1)
             def _():
                 send_left(at_left).wait_recv()
-                left_out[at_left] = (
-                    part[at_left] + after[at_left].astype(jnp.float32)
-                ).astype(left_out.dtype)
+                for cut, spot in halves(at_left):
+                    left_out[at_left, cut] = (
+                        part[spot] + after[at_left, cut].astype(jnp.float32)
+                    ).astype(left_out.dtype)
 
             send_left(at_left).start()
 
@@ -1049,12 +1115,20 @@
         @pl.when(at_total >= 0)
         def _():
             chunk = at_total // quarters
-            quarter = lax.rem(at_total, quarters)
-
-            @pl.when(jnp.logical_and(quarter == 0, chunk > 0))
+            turn = lax.rem(at_total, quarters)
+
+            @pl.when(
+                jnp.logical_and(
+                    jnp.logical_and(turn == 0, chunk > 0), jnp.logical_or(chunk <= split_from, core == 1)
+                )
+            )
             def _():
                 settle(chunk - 1)
 
+            @pl.when(jnp.logical_and(jnp.logical_and(turn == 2, chunk >= split_from), core == 0))
+            def _():
+                settle(chunk)
+
             @pl.when(me == line - 1)
             def _():
                 send_right(at_total).wait_recv()
@@ -1063,38 +1137,60 @@
             def _():
                 send_left(at_total).wait_recv()
 
-            @pl.when(me > 0)
-            def _():
-                part[at_total] = part[at_total] + before[at_total].astype(jnp.float32)
-
-            @pl.when(me < line - 1)
-            def _():
-                part[at_total] = part[at_total] + after[at_total].astype(jnp.float32)
-
-            value = part[at_total] + b1_ref[...].reshape(1, -1).astype(jnp.float32)
-            value = 0.5 * value * (1.0 + lax.erf(value * HALF_ROOT))
-            hidden[chunk, chip_of(quarter)] = value.astype(hidden.dtype).reshape(hidden.shape[2:])
-
-            @pl.when(quarter == quarters - 1)
-            def _():
-                for_pair = hidden[chunk, :, :, 1 - core].reshape(-1, hidden.shape[5])
-                for_me = hidden[chunk, :, :, core].reshape(-1, hidden.shape[5])
-                count = for_me.shape[0]
-                lhs = jnp.concatenate([for_pair, for_me], axis=0)
+            for cut, spot in halves(at_total):
+                _, quarter, target = spot
+
+                @pl.when(me > 0)
+                def _():
+                    part[spot] = part[spot] + before[at_total, cut].astype(jnp.float32)
+
+                @pl.when(me < line - 1)
+                def _():
+                    part[spot] = part[spot] + after[at_total, cut].astype(jnp.float32)
+
+                value = part[spot] + b1_ref[...].reshape(1, -1).astype(jnp.float32)
+                value = 0.5 * value * (1.0 + lax.erf(value * HALF_ROOT))
+                hidden[chunk, target, chip_of(quarter)] = value.astype(hidden.dtype)
+
+            def project(target):
+                lhs = hidden[chunk, target].reshape(-1, hidden.shape[4])
 
                 @pl.loop(0, w2_ref.shape[1] // FC2_COLS)
                 def _(at):
                     cols = pl.ds(pl.multiple_of(at * FC2_COLS, FC2_COLS), FC2_COLS)
                     result = jnp.dot(lhs, w2_ref[:, cols], preferred_element_type=jnp.float32)
-                    give[chunk, :, cols] = result[:count].astype(give.dtype)
-                    keep[chunk, :, cols] = result[count:]
-
-                send_give(chunk).start()
+
+                    @pl.when(core == target)
+                    def _():
+                        keep[chunk, :, cols] = result
+
+                    @pl.when(core != target)
+                    def _():
+                        give[chunk, :, cols] = result.astype(give.dtype)
+
+                @pl.when(core != target)
+                def _():
+                    send_give(chunk).start()
+
+            @pl.when(jnp.logical_and(turn == 1, chunk >= split_from))
+            def _():
+                project(0)
+
+            @pl.when(turn == quarters - 1)
+            def _():
+                @pl.when(chunk < split_from)
+                def _():
+                    project(0)
+
+                project(1)
 
         return carry
 
     lax.fori_loop(0, pieces + 1 + lag_total, stage, 0)
-    settle(chips - 1)
+
+    @pl.when(core == 1)
+    def _():
+        settle(chips - 1)
 
     spot_sum = spots[0]
     for copy in place_copies:
@@ -1156,8 +1252,8 @@
         exchange(step).wait_send()
 
     for chunk in range(chips):
-        for copy in own_sends(chunk):
-            copy.wait_send()
+        for which in range(3):
+            own_send(chunk, which).wait_send()
         forward_x(chunk).wait_send()
         for quarter in range(1, quarters):
             forward_pair(chunk, quarter).wait_send()
@@ -1230,11 +1326,14 @@
             jax.ShapeDtypeStruct(carry.shape, carry.dtype),
         ),
         in_specs=[
-            pl.BlockSpec(memory_space={1: pltpu.SMEM, 7: pl.ANY, 9: pl.ANY, 11: pl.ANY, 12: pl.ANY}.get(at, pltpu.VMEM))
+            pl.BlockSpec(memory_space={1: pltpu.SMEM, 2: pltpu.VMEM, 5: pltpu.VMEM, 6: pltpu.VMEM, 8: pltpu.VMEM, 10: pltpu.VMEM}.get(at, pl.ANY))
             for at in range(13)
         ],
         out_specs=[pl.BlockSpec(memory_space=pltpu.VMEM)] * 4 + [pl.BlockSpec(memory_space=pl.ANY)],
         scratch_shapes=[
+            pltpu.VMEM(patches.shape, low),
+            pltpu.VMEM(qkv.shape, low),
+            pltpu.VMEM(wo.shape, low),
             pltpu.VMEM(text.shape, low),
             pltpu.VMEM(text.shape, low),
             pltpu.VMEM((text.shape[0], 128), jnp.float32),
@@ -1255,7 +1354,7 @@
             pltpu.VMEM((chips, chunk_rows, width), low),
             pltpu.VMEM(w1.shape, low),
             pltpu.VMEM(w2.shape, low),
-            dma((2,)),
+            dma((5,)),
             dma((line - 1,)),
             dma((line - 1,)),
             dma((line - 1, 7)),
@@ -1264,12 +1363,12 @@
             dma((line - 1,)),
             dma((line - 1,)),
             pltpu.VMEM((groups, chips, chunk_rows, width), low),
-            pltpu.VMEM((pieces, piece_rows, units), jnp.float32),
+            pltpu.VMEM((chips, 4, 2, chunk_rows, units), jnp.float32),
             pltpu.VMEM((pieces, piece_rows, units), low),
             pltpu.VMEM((pieces, piece_rows, units), low),
             pltpu.VMEM((pieces, piece_rows, units), low),
             pltpu.VMEM((pieces, piece_rows, units), low),
-            pltpu.VMEM((chips, chips, 2, 2, run, units), low),
+            pltpu.VMEM((chips, 2, chips, chunk_rows, units), low),
             pltpu.VMEM((chips, target_rows, features), low),
             pltpu.VMEM((chips, target_rows, features), low),
             pltpu.VMEM((chips, target_rows, features), jnp.float32),

time: 114 us -> 108 us (0.947)
  Pallas kernels: 113 us -> 106 us
    pallas_call x1, Pallas kernels: 108 us -> 101 us  [merger(): pl.pallas_call(merger_kernel, out_shape=(jax.ShapeDtypeStruct((target_row...]
where the time goes in v4:
time: 108 us; the launch traced here: 107 us
  Pallas kernels  106 us (98%)
    pallas_call x1, Pallas kernels, merger(): pl.pallas_call(merger_kernel, out_shape=(jax.ShapeDtypeStruct((target_row...  101 us
    pallas_call x1, Pallas kernels, placing(): pl.pallas_call(placing_kernel, out_shape=(jax.ShapeDtypeStruct(text.shape...  5.02 us

profile of v4, /device:TPU:0, one launch (start us, length us, event | category | flops | bytes accessed | tf_op | source)
XLA Modules:
  0.0 106.6 jit_solution(14154048262559305736)
XLA Ops:
  0.6 101.0 %shard_map.149 = (bf16[128,2048]{1,0:T(8,128)(2,1)}, s32[1,128]{1,0:T(1,128)}, f32[4,128]{1,0:T(4,128)}, f32[1,128]{1,0:T(1,128)}, bf16[512,2048]{1,0:T(8,128)(2,1)}) custom-call(bf16[512,1280]{1,0:T(8,128)(2,1)} %patches_hbm.1, s32[2]{0:T(128)} %counts_ref.1, s32[128]{0:T(128)} %dest_ref.1, bf16[3,320,1280]{2,1,0:T(8,128)(2,1)} %bitcast.1, ...), custom_call_target="tpu_custom_call" | custom-call | flops 99999997952 | bytes 10000000 | tf_op jit(solution)/shard_map/pallas_call | solution.py:1319
  101.6 5.0 %shard_map.150 = (bf16[512,2048]{1,0:T(8,128)(2,1)}, bf16[512,2048]{1,0:T(8,128)(2,1)}) custom-call(bf16[512,2048]{1,0:T(8,128)(2,1)} %text_hbm.3, bf16[512,2048]{1,0:T(8,128)(2,1)} %get-tuple-element.7.incoming_hbm, bf16[128,2048]{1,0:T(8,128)(2,1)} %get-tuple-element.8.img_ref, s32[1,128]{1,0:T(1,128)} %get-tuple-element.9.spot_ref, ...), custom_call_target="tpu_custom_call" | custom-call | flops 1000000000 | bytes 10000000 | tf_op jit(solution)/shard_map/pallas_call | solution.py:1494

commit v5 on v4

--- a/solution.py
+++ b/solution.py
@@ -484,8 +484,8 @@
     return (sequence_embeds, layer_inputs)
 
 
-LAG = 3
-FC2_COLS = 512
+LAG = 2
+FC2_COLS = 1024
 HALF_ROOT = 0.5**0.5
 
 
@@ -625,8 +625,8 @@
     take_rows = rows.shape[2] // 2
     lag_right = me * LAG
     half_rows = part.shape[3]
-    split_from = 2
-    single = 6
+    split_from = 3
+    single = 8
     run = half_rows // 2
     lag_left = (line - 1 - me) * LAG
     lag_total = (line - 1) * LAG
@@ -845,37 +845,44 @@
             result = result + jnp.dot(weights, tile_value * own, preferred_element_type=jnp.float32)
         attended[cut] = result.astype(attended.dtype)
 
+    tile_slots = slots // tiles
+
+    def pick(height, width, patch):
+        at_row = lax.broadcasted_iota(jnp.int32, (height, width), 0)
+        at_patch = lax.broadcasted_iota(jnp.int32, (height, width), 1)
+        return (at_patch == at_row * line + patch).astype(jnp.float32).astype(jnp.bfloat16)
+
+    def exchange(step, tile):
+        peer = lax.rem(me + step, line)
+        cut = pl.ds(tile * tile_slots, tile_slots)
+        return remote(
+            ordered.at[peer, cut], arrived.at[me, cut], a_send.at[step - 1, tile], a_recv.at[step - 1, tile], {"mp": peer}
+        )
+
+    def spread(tile):
+        source = attended[pl.ds(tile * block, block)]
+        for patch in range(line):
+            ordered[patch, pl.ds(tile * tile_slots, tile_slots)] = jnp.dot(
+                pick(tile_slots, block, patch), source, preferred_element_type=jnp.float32
+            ).astype(ordered.dtype)
+        for step in (first_sent, second, last_sent):
+            exchange(step, tile).start()
+
     for tile in range(tiles):
         attend(tile)
+        spread(tile)
         if tile == 0:
             begin(second)
+    begin(last_here)
     pass_y(first_here)
-    begin(last_here)
     send_bands(early, bands - looped)
-
-    whole = attended.shape[0]
-    at_row = lax.broadcasted_iota(jnp.int32, (slots, whole), 0)
-    at_patch = lax.broadcasted_iota(jnp.int32, (slots, whole), 1)
+    arrived[me] = ordered[me]
     order = (
         lax.broadcasted_iota(jnp.int32, (slots, slots), 0) == slot_target
     ).astype(jnp.float32).astype(jnp.bfloat16)
-
-    def picked(patch, source):
-        pick = (at_patch == at_row * line + patch).astype(jnp.float32).astype(jnp.bfloat16)
-        rows_of = jnp.dot(pick, source, preferred_element_type=jnp.float32).astype(jnp.bfloat16)
-        return jnp.dot(order, rows_of, preferred_element_type=jnp.float32)
-
-    for patch in range(line):
-        ordered[patch] = picked(patch, attended[...]).astype(ordered.dtype)
-
-    def exchange(step):
-        peer = lax.rem(me + step, line)
-        return remote(ordered.at[peer], arrived.at[me], a_send.at[step - 1], a_recv.at[step - 1], {"mp": peer})
-
-    for step in steps:
-        exchange(step).start()
-    arrived[me] = ordered[me]
-    block_out = picked(me, patches_ref[...])
+    block_out = jnp.dot(
+        pick(slots, patches_ref.shape[0], me), patches_ref[...], preferred_element_type=jnp.float32
+    )
     pass_y(second)
     pass_x(first_here, 2)
     pass_y(last_here)
@@ -888,14 +895,16 @@
         for quarter in range(quarters):
             wo_paired(step, quarter).wait_recv()
     for step in steps:
-        exchange(step).wait_recv()
+        for tile in range(tiles):
+            exchange(step, tile).wait_recv()
     for source in range(line):
         block_out = block_out + jnp.dot(
             arrived[source], wo_all[source], preferred_element_type=jnp.float32
         )
     block_out = block_out.astype(jnp.bfloat16)
+    merged = layer_norm(block_out, merge_gain_ref[...].reshape(1, -1)).astype(x_ref.dtype)
     x_ref[...] = (
-        layer_norm(block_out, merge_gain_ref[...].reshape(1, -1)).astype(x_ref.dtype).reshape(x_ref.shape)
+        jnp.dot(order, merged, preferred_element_type=jnp.float32).astype(x_ref.dtype).reshape(x_ref.shape)
     )
     for chunk in range(chips):
         own_send(chunk, 0).start()
@@ -1249,7 +1258,8 @@
             copy.wait_send()
         for quarter in range(1, quarters):
             wo_forward_pair(step, quarter).wait_send()
-        exchange(step).wait_send()
+        for tile in range(tiles):
+            exchange(step, tile).wait_send()
 
     for chunk in range(chips):
         for which in range(3):
@@ -1311,7 +1321,7 @@
     pieces = chips * 4
     piece_rows = 2 * chunk_rows
     target_rows = groups * run
-    parts = 4
+    parts = 8
     low = jnp.bfloat16
     dma = pltpu.SemaphoreType.DMA
     sum_rows = text.shape[0] // 128
@@ -1360,8 +1370,8 @@
             dma((line - 1, 7)),
             dma((line - 1, 4)),
             dma((line - 1, 4)),
-            dma((line - 1,)),
-            dma((line - 1,)),
+            dma((line - 1, counts.shape[0])),
+            dma((line - 1, counts.shape[0])),
             pltpu.VMEM((groups, chips, chunk_rows, width), low),
             pltpu.VMEM((chips, 4, 2, chunk_rows, units), jnp.float32),
             pltpu.VMEM((pieces, piece_rows, units), low),
@@ -1430,8 +1440,9 @@
     load_sem,
     store_sem,
 ):
-    cuts = base_ref.shape[0]
+    cuts = load_sem.shape[1]
     height = text.shape[0] // cuts
+    per = base_ref.shape[1] // height
     first = lax.axis_index("section") == 0
     gain = gain_ref[...].reshape(1, -1).astype(jnp.float32)
 
@@ -1453,9 +1464,8 @@
             move(1, at).start()
 
     width = base_ref.shape[1]
-    diagonal = lax.broadcasted_iota(jnp.int32, (height, width), 0) == lax.broadcasted_iota(
-        jnp.int32, (height, width), 1
-    )
+    lane = lax.broadcasted_iota(jnp.int32, (height, width), 1)
+    low_row = lax.broadcasted_iota(jnp.int32, (height, width), 0)
     for at in range(cuts):
         cut = pl.ds(at * height, height)
         at_row = at * height + lax.broadcasted_iota(jnp.int32, (height, spot_ref.shape[1]), 0)
@@ -1464,7 +1474,10 @@
         placed = jnp.dot(
             hits.astype(jnp.float32).astype(jnp.bfloat16), img_ref[...], preferred_element_type=jnp.float32
         ).astype(jnp.bfloat16)
-        base = jnp.sum(jnp.where(diagonal, base_ref[at : at + 1], 0.0), axis=1, keepdims=True)
+        diagonal = lane == low_row + at % per * height
+        base = jnp.sum(
+            jnp.where(diagonal, base_ref[at // per : at // per + 1], 0.0), axis=1, keepdims=True
+        )
         move(0, at).wait()
         seq[cut] = jnp.where(hit, placed, text[cut])
         move(2, at).start()

time: 108 us -> 106 us (0.981); the launches traced: 107 us -> 106 us
  no operation moved by 1% of the time
where the time goes in v5:
time: 106 us
  Pallas kernels  105 us (99%)
    pallas_call x1, Pallas kernels, merger(): pl.pallas_call(merger_kernel, out_shape=(jax.ShapeDtypeStruct((target_row...  100 us
    pallas_call x1, Pallas kernels, placing(): pl.pallas_call(placing_kernel, out_shape=(jax.ShapeDtypeStruct(text.shape...  5.03 us

profile of v5, /device:TPU:0, one launch (start us, length us, event | category | flops | bytes accessed | tf_op | source)
XLA Modules:
  0.0 106.0 jit_solution(14276478848249696387)
XLA Ops:
  0.6 100.3 %shard_map.149 = (bf16[128,2048]{1,0:T(8,128)(2,1)}, s32[1,128]{1,0:T(1,128)}, f32[4,128]{1,0:T(4,128)}, f32[1,128]{1,0:T(1,128)}, bf16[512,2048]{1,0:T(8,128)(2,1)}) custom-call(bf16[512,1280]{1,0:T(8,128)(2,1)} %patches_hbm.1, s32[2]{0:T(128)} %counts_ref.1, s32[128]{0:T(128)} %dest_ref.1, bf16[3,320,1280]{2,1,0:T(8,128)(2,1)} %bitcast.1, ...), custom_call_target="tpu_custom_call" | custom-call | flops 99999997952 | bytes 10000000 | tf_op jit(solution)/shard_map/pallas_call | solution.py:1329
  100.9 5.0 %shard_map.150 = (bf16[512,2048]{1,0:T(8,128)(2,1)}, bf16[512,2048]{1,0:T(8,128)(2,1)}) custom-call(bf16[512,2048]{1,0:T(8,128)(2,1)} %text_hbm.3, bf16[512,2048]{1,0:T(8,128)(2,1)} %get-tuple-element.7.incoming_hbm, bf16[128,2048]{1,0:T(8,128)(2,1)} %get-tuple-element.8.img_ref, s32[1,128]{1,0:T(1,128)} %get-tuple-element.9.spot_ref, ...), custom_call_target="tpu_custom_call" | custom-call | flops 1000000000 | bytes 10000000 | tf_op jit(solution)/shard_map/pallas_call | solution.py:1507

commit v6 on v5

--- a/solution.py
+++ b/solution.py
@@ -626,7 +626,7 @@
     lag_right = me * LAG
     half_rows = part.shape[3]
     split_from = 3
-    single = 8
+    single = 12
     run = half_rows // 2
     lag_left = (line - 1 - me) * LAG
     lag_total = (line - 1) * LAG

time: 106 us -> 117 us (1.10)
  Pallas kernels: 105 us -> 116 us
    pallas_call x1, Pallas kernels: 100 us -> 111 us  [merger(): pl.pallas_call(merger_kernel, out_shape=(jax.ShapeDtypeStruct((target_row...]
where the time goes in v6:
time: 117 us; the launch traced here: 116 us
  Pallas kernels  116 us (99%)
    pallas_call x1, Pallas kernels, merger(): pl.pallas_call(merger_kernel, out_shape=(jax.ShapeDtypeStruct((target_row...  111 us
    pallas_call x1, Pallas kernels, placing(): pl.pallas_call(placing_kernel, out_shape=(jax.ShapeDtypeStruct(text.shape...  5.03 us

profile of v6, /device:TPU:0, one launch (start us, length us, event | category | flops | bytes accessed | tf_op | source)
XLA Modules:
  0.0 116.4 jit_solution(3977832903256177560)
XLA Ops:
  0.6 110.7 %shard_map.149 = (bf16[128,2048]{1,0:T(8,128)(2,1)}, s32[1,128]{1,0:T(1,128)}, f32[4,128]{1,0:T(4,128)}, f32[1,128]{1,0:T(1,128)}, bf16[512,2048]{1,0:T(8,128)(2,1)}) custom-call(bf16[512,1280]{1,0:T(8,128)(2,1)} %patches_hbm.1, s32[2]{0:T(128)} %counts_ref.1, s32[128]{0:T(128)} %dest_ref.1, bf16[3,320,1280]{2,1,0:T(8,128)(2,1)} %bitcast.1, ...), custom_call_target="tpu_custom_call" | custom-call | flops 99999997952 | bytes 10000000 | tf_op jit(solution)/shard_map/pallas_call | solution.py:1329
  111.3 5.0 %shard_map.150 = (bf16[512,2048]{1,0:T(8,128)(2,1)}, bf16[512,2048]{1,0:T(8,128)(2,1)}) custom-call(bf16[512,2048]{1,0:T(8,128)(2,1)} %text_hbm.3, bf16[512,2048]{1,0:T(8,128)(2,1)} %get-tuple-element.7.incoming_hbm, bf16[128,2048]{1,0:T(8,128)(2,1)} %get-tuple-element.8.img_ref, s32[1,128]{1,0:T(1,128)} %get-tuple-element.9.spot_ref, ...), custom_call_target="tpu_custom_call" | custom-call | flops 1000000000 | bytes 10000000 | tf_op jit(solution)/shard_map/pallas_call | solution.py:1507
